TPU v7x, 128 devices: a whole 4x4x4 slice. The times are simulated.
128 devices in a mesh: data: 1, feat: 2 (over core), graph: 64 (over z, y, x).
Axes of the slice: x: 4, y: 4, z: 4, core: 2. Of those that a mesh axis runs over, the one named last changes fastest.
Arguments:
- X: bfloat16 [131072, 100], P(('data', 'graph'), 'feat')
- dst_local: int32 [6553600], P(('data', 'graph'))
- src_slot: int32 [6553600], P(('data', 'graph'))
- valid: int32 [6553600], P(('data', 'graph'))
- w: float32 [6553600], P(('data', 'graph'))
- send_idx: int32 [4096, 32], P(('data', 'graph'))
- send_valid: int32 [4096, 32], P(('data', 'graph'))
- hub_ids: int32 [1024], P('data')
- W1: bfloat16 [100, 256], P('feat')
- W2: bfloat16 [256, 256], P('feat')
- b1: float32 [256], P('feat')
- b2: float32 [256], P('feat')
Outputs:
- output: float32 [131072, 256], P(('data', 'graph'), 'feat')
All inputs are finite; a program needn't handle non-finite values.
Results may differ from a plain program's by a relative error of at most 0.001.
Values are sent between devices in bfloat16 or wider.
A program may use at most 1 GiB of HBM per device.

v0:
```python
import functools

import jax
import jax.numpy as jnp
from jax import lax
from jax.experimental import pallas as pl
from jax.experimental.pallas import tpu as pltpu
from jax.sharding import PartitionSpec as P


DB = 128
SB = 256
CH = 256
LANES = 128
UNROLL = 8
BF = jnp.bfloat16
F32 = jnp.float32
VMEM_LIMIT = 56 << 20


def over(a, n):
    return lax.shift_right_arithmetic(a, n.bit_length() - 1)


def split3(a):
    hi = a.astype(BF)
    rest = a - hi.astype(F32)
    mid = rest.astype(BF)
    low = (rest - mid.astype(F32)).astype(BF)
    return hi, mid, low


def product(load, table_ref):
    depth, _ = table_ref.shape
    total = None
    for k in range(0, depth, SB):
        pieces = jnp.concatenate(split3(load(k)), axis=0)
        part = jnp.dot(pieces, table_ref[k : k + SB, :], preferred_element_type=F32)
        total = part if total is None else total + part
    rows = total.shape[0] // 3
    return total[:rows] + total[rows : 2 * rows] + total[2 * rows :]


def store_halves(y, mine_ref, other_ref):
    width = mine_ref.shape[1]
    mine_ref[...] = y[:, :width]
    other_ref[...] = y[:, width:]


def build_kernel(n_src, first_block, kf_ref, kl_ref, begin_ref, key_ref, low_ref, w_ref, table_ref, a_ref, mine_ref, other_ref, state_ref):
    step = pl.program_id(0)
    n_chunks = key_ref.shape[0]
    per = CH // LANES

    @pl.when(step == 0)
    def _():
        state_ref[0] = begin_ref[0]
        state_ref[1] = begin_ref[1]

    first = (first_block + step) * n_src
    limit = first + n_src
    a_ref[...] = jnp.zeros_like(a_ref)

    def body(carry):
        chunk, bucket = carry
        for _ in range(UNROLL):
            live = bucket < limit
            here = jnp.minimum(chunk, n_chunks - 1)
            lows = low_ref[here]
            match = key_ref[here] == jnp.where(live, bucket, -1)
            d_low = jnp.where(match, lax.shift_right_logical(lows, 8), -1)
            s_low = lows & (SB - 1)
            d_mask = lax.broadcasted_iota(jnp.int32, (DB, CH), 0) == d_low
            pieces = [jnp.where(d_mask, piece.astype(F32), 0.0).astype(BF) for piece in split3(w_ref[here])]
            s_hot = jnp.where(lax.broadcasted_iota(jnp.int32, (SB, CH), 0) == s_low, 1.0, 0.0).astype(BF)
            got = lax.dot_general(
                jnp.concatenate(pieces, axis=0), s_hot, (((1,), (1,)), ((), ())), preferred_element_type=F32
            )
            got = got[:DB] + got[DB : 2 * DB] + got[2 * DB :]
            column = pl.multiple_of(jnp.clip(bucket - first, 0, n_src - 1) * SB, SB)
            a_ref[:, pl.ds(column, SB)] += got
            done = bucket >= kl_ref[here * per + per - 1]
            next_chunk = chunk + jnp.where(done, 1, 0)
            next_bucket = jnp.where(done, kf_ref[next_chunk * per], bucket + 1)
            chunk = jnp.where(live, next_chunk, chunk)
            bucket = jnp.where(live, next_bucket, bucket)
        return chunk, bucket

    chunk, bucket = lax.while_loop(lambda c: c[1] < limit, body, (state_ref[0], state_ref[1]))
    state_ref[0] = chunk
    state_ref[1] = bucket
    store_halves(product(lambda k: a_ref[:, k : k + SB], table_ref), mine_ref, other_ref)


def build_and_multiply(edges, begin, table, first_block, n_blocks):
    k_first, k_last, keys, low, w = edges
    depth, full = table.shape
    n_src = depth // SB
    n_chunks = keys.shape[0]
    whole = lambda *shape: pl.BlockSpec(shape, lambda i, *_: (0,) * len(shape), pipeline_mode=pl.Buffered(1))
    rows = n_blocks * DB
    half = pl.BlockSpec((DB, full // 2), lambda i, *_: (i, 0))
    return pl.pallas_call(
        functools.partial(build_kernel, n_src, first_block),
        grid_spec=pltpu.PrefetchScalarGridSpec(
            num_scalar_prefetch=3,
            grid=(n_blocks,),
            in_specs=[whole(n_chunks, 1, CH)] * 3 + [whole(depth, full)],
            out_specs=[
                pl.BlockSpec((DB, depth), lambda i, *_: (i, 0)),
                half,
                half,
                pl.BlockSpec(memory_space=pltpu.SMEM),
            ],
        ),
        out_shape=[
            jax.ShapeDtypeStruct((rows, depth), F32),
            jax.ShapeDtypeStruct((rows, full // 2), F32),
            jax.ShapeDtypeStruct((rows, full // 2), F32),
            jax.ShapeDtypeStruct((2,), jnp.int32),
        ],
        compiler_params=pltpu.CompilerParams(dimension_semantics=("arbitrary",), vmem_limit_bytes=VMEM_LIMIT),
        cost_estimate=pl.CostEstimate(flops=n_blocks * 2 * 10**9, bytes_accessed=8 * rows * depth, transcendentals=0),
        name="build_adjacency",
    )(k_first, k_last, begin, keys, low, w, table)


def multiply_kernel(*refs):
    *a_refs, table_ref, mine_ref, other_ref = refs
    cols = a_refs[0].shape[1]
    load = lambda k: a_refs[k // cols][:, k % cols : k % cols + SB]
    store_halves(product(load, table_ref), mine_ref, other_ref)


def multiply(a, table):
    rows, depth = a.shape
    full = table.shape[1]
    cols = 2 * SB
    tall = 2 * DB
    half = pl.BlockSpec((tall, full // 2), lambda i: (i, 0))
    strip = lambda j: pl.BlockSpec((tall, cols), lambda i: (i, j))
    n_strips = depth // cols
    return pl.pallas_call(
        multiply_kernel,
        grid=(rows // tall,),
        in_specs=[strip(j) for j in range(n_strips)]
        + [pl.BlockSpec((depth, full), lambda i: (0, 0), pipeline_mode=pl.Buffered(1))],
        out_specs=[half, half],
        out_shape=[jax.ShapeDtypeStruct((rows, full // 2), F32)] * 2,
        compiler_params=pltpu.CompilerParams(dimension_semantics=("arbitrary",), vmem_limit_bytes=VMEM_LIMIT),
        cost_estimate=pl.CostEstimate(flops=6 * rows * depth * full, bytes_accessed=4 * rows * depth, transcendentals=0),
        name="multiply_adjacency",
    )(*[a] * n_strips, table)


def solution(mesh):
    rows_axes = ("data", "graph")
    n_graph = mesh.shape["graph"]
    swap = [(0, 1), (1, 0)]

    def device_program(x_loc, dst, src, valid, w, send_idx, send_valid, hub_ids, w_first, w_second, b_first, b_second):
        verts = x_loc.shape[0]
        hubs = hub_ids.shape[0]
        own_hubs = hubs // n_graph
        halo = send_idx.shape[1]
        width = b_first.shape[0]
        me = lax.axis_index("graph")
        col = lax.axis_index("feat")
        v_half, s_half, k_half = verts // 2, halo // 2, hubs // 2
        depth = v_half + n_graph * s_half + k_half
        n_src = depth // SB
        hub_blocks, local_blocks = hubs // DB, verts // DB
        none = (hub_blocks + local_blocks) * n_src

        def columns_of(weight):
            mine = lax.dynamic_slice_in_dim(weight, col * width, width, 1)
            theirs = lax.dynamic_slice_in_dim(weight, (1 - col) * width, width, 1)
            weight = jnp.concatenate([mine, theirs], axis=1)
            other = lax.ppermute(weight, "feat", swap)
            return weight, jnp.concatenate([other[:, width:], other[:, :width]], axis=1)

        w1 = columns_of(w_first)
        w2 = columns_of(w_second)

        in_halo = src - verts
        in_hub = in_halo - n_graph * halo
        is_own, is_halo = in_halo < 0, in_hub < 0
        half = jnp.where(is_own, over(src, v_half), jnp.where(is_halo, over(in_halo & (halo - 1), s_half), over(in_hub, k_half)))
        row = jnp.where(
            is_own,
            src & (v_half - 1),
            jnp.where(
                is_halo,
                v_half + over(in_halo, halo) * s_half + (in_halo & (s_half - 1)),
                v_half + n_graph * s_half + (in_hub & (k_half - 1)),
            ),
        )
        target = jnp.where(dst >= verts, dst - verts, dst + hubs)
        bucket = lax.shift_right_logical(target, 7) * n_src + lax.shift_right_logical(row, 8)
        n_edges = dst.shape[0]
        padded = -(-max(n_edges, 131072) // CH) * CH
        fill = (0, padded - n_edges)
        key = jnp.pad(jnp.where((valid > 0) & (half == col), bucket, none), fill, constant_values=none)
        low = jnp.pad((target & (DB - 1)) * SB + (row & (SB - 1)), fill)
        key, low, w_sorted = lax.sort((key, low, jnp.pad(w, fill)), num_keys=1, is_stable=False)
        key_rows = key.reshape(-1, LANES)
        end = jnp.full((8,), none, jnp.int32)
        k_first = jnp.concatenate([jnp.min(key_rows, axis=1), end])
        k_last = jnp.concatenate([jnp.max(key_rows, axis=1), end])
        chunks = lambda a: a.reshape(padded // CH, 1, CH)
        edges = (k_first, k_last, chunks(key), chunks(low), chunks(w_sorted))

        owner = over(hub_ids, verts)
        ids = jnp.arange(hubs)
        earlier = (owner[None, :] == owner[:, None]) & (ids[None, :] < ids[:, None])
        place = owner * own_hubs + jnp.sum(earlier.astype(jnp.int32), axis=1)
        place_half = lax.dynamic_slice_in_dim(place, col * k_half, k_half)
        hub_hot = (place_half[:, None] == ids[None, :]).astype(BF)
        hub_hot_t = (place[None, :] == ids[:, None]).astype(BF)
        slot_ids = me * own_hubs + jnp.arange(own_hubs)
        my_rows = jnp.sum(jnp.where(place[None, :] == slot_ids[:, None], hub_ids[None, :], 0), axis=1) - me * verts

        wanted = jnp.where(send_valid > 0, send_idx, -1)
        wanted = lax.dynamic_slice_in_dim(wanted, col * s_half, s_half, 1)
        wanted = jnp.concatenate([wanted, jnp.broadcast_to(my_rows[None, :], (n_graph, own_hubs))], axis=1)
        wanted = wanted.reshape(-1)
        send_hot = (wanted[:, None] == jnp.arange(verts)[None, :]).astype(BF)

        def table_of(mine, weights):
            other = lax.ppermute(mine, "feat", swap)
            z = jnp.dot(mine, weights[0], preferred_element_type=F32)
            z = (z + jnp.dot(other, weights[1], preferred_element_type=F32)).astype(BF)
            out = jnp.dot(send_hot, z, preferred_element_type=F32).astype(BF)
            got = lax.all_to_all(out.reshape(n_graph, s_half + own_hubs, 2 * width), "graph", 0, 0, tiled=True)
            hub_rows = got[:, s_half:].reshape(hubs, 2 * width)
            hub_rows = jnp.dot(hub_hot, hub_rows, preferred_element_type=F32).astype(BF)
            own = lax.dynamic_slice_in_dim(z, col * v_half, v_half)
            return jnp.concatenate([own, got[:, :s_half].reshape(n_graph * s_half, 2 * width), hub_rows], axis=0)

        def hub_parts(mine, other):
            sums = mine + lax.ppermute(other, "feat", swap)
            hi = lax.reduce_precision(sums, 8, 7)
            mid = lax.reduce_precision(sums - hi, 8, 7)
            pieces = jnp.concatenate([hi.astype(BF), mid.astype(BF), ((sums - hi) - mid).astype(BF)], axis=1)
            got = jnp.dot(hub_hot_t, pieces, preferred_element_type=F32)
            return got[:, :width] + got[:, width : 2 * width] + got[:, 2 * width :]

        def hub_total(parts):
            got = lax.all_to_all(parts.reshape(n_graph, own_hubs, width), "graph", 0, 0, tiled=True)
            return jnp.sum(got, axis=0)

        def finish(mine, other, total, bias):
            return (mine + lax.ppermute(other, "feat", swap) + bias).at[my_rows].add(total)

        table = table_of(x_loc, w1)
        begin = jnp.stack([jnp.int32(0), k_first[0]])
        a_hub, mine, other, state = build_and_multiply(edges, begin, table, 0, hub_blocks)
        parts, state = lax.optimization_barrier((hub_parts(mine, other), state))
        total = hub_total(parts)
        a_local, mine, other, _ = build_and_multiply(edges, state, table, hub_blocks, local_blocks)
        hidden = jnp.maximum(finish(mine, other, total, b_first), 0.0).astype(BF)

        table = table_of(hidden, w2)
        parts, table_local = lax.optimization_barrier((hub_parts(*multiply(a_hub, table)), table))
        total = hub_total(parts)
        mine, other = multiply(a_local, table_local)
        return finish(mine, other, total, b_second)

    edge = P(rows_axes)
    send = P(rows_axes, None)
    in_specs = (P(rows_axes, "feat"), edge, edge, edge, edge, send, send, P("data"), P("feat", None), P("feat", None), P("feat"), P("feat"))
    return jax.shard_map(device_program, mesh=mesh, in_specs=in_specs, out_specs=P(rows_axes, "feat"), check_vma=False)
```

profile of v0, /device:TPU:0, one launch (start us, length us, event | category | flops | bytes accessed | tf_op | source)
XLA Modules:
  0.0 240.5 jit_solution(14685355082876592855)
XLA Ops:
  6.5 0.8 constant_dynamic-slice_fusion.4
  7.3 0.1 collective-permute-start
  7.4 0.5 collective-permute-start.1
  7.9 1.7 and_add_fusion
  9.7 0.0 copy-start.3
  9.7 0.8 pad.14
  10.5 0.8 pad.15
  11.3 0.9 pad.13
  12.2 0.0 sort.23.cloned.1.call-update
  12.2 0.5 fusion.42
  12.7 0.1 copy-done.5
  12.9 0.5 convert_reduce_fusion
  13.4 0.2 select_reduce_fusion
  13.6 0.1 pad.33.clone
  13.7 0.1 pad_add_fusion
  13.8 0.1 copy.20
  13.9 0.1 eq.81
  14.0 0.5 fusion.7
  14.5 3.8 %fusion.9 = bf16[2048,256]{1,0:T(8,128)(2,1)} fusion(bf16[256,2048]{0,1:T(8,128)(2,1)S(1)} %fusion.7, s32[2048]{0:T(1024)S(1)} %eq.81), kind=kOutput, calls=%fused_computation.17 | convolution fusion | flops 2152202240 | bytes 2105344 | tf_op jit(solution)/shard_map/dot_general | solution.py:233
  18.3 11.5 %all-to-all-start = ((bf16[64,32,256]{2,1,0:T(8,128)(2,1)}), bf16[64,32,256]{2,1,0:T(8,128)(2,1)S(1)}, u32[]{:S(2)}, u32[]{:S(2)}) async-start(bf16[64,32,256]{2,1,0:T(8,128)(2,1)} %bitcast.5), calls=%async_computation | async-start | bytes 2097152 | tf_op jit(solution)/shard_map/all_to_all | solution.py:234
  29.8 0.1 dynamic_slice.28
  29.9 19.0 %all-to-all-done = bf16[64,32,256]{2,1,0:T(8,128)(2,1)S(1)} async-done(((bf16[64,32,256]{2,1,0:T(8,128)(2,1)}), bf16[64,32,256]{2,1,0:T(8,128)(2,1)S(1)}, u32[]{:S(2)}, u32[]{:S(2)}) %all-to-all-start) | async-done | bytes 1048608 | tf_op jit(solution)/shard_map/all_to_all | solution.py:234
  49.0 0.1 fusion.45
  49.1 0.5 fusion.15
  49.6 1.2 pad_maximum_fusion.table_ref
  50.8 1.4 bitcast_reduce_fusion
  52.1 0.5 slice.45
  52.7 0.6 concatenate.33.kf_ref
  53.3 0.6 concatenate.34.kl_ref
  53.9 1.2 pad_add_fusion.1.begin_ref
  55.1 20.4 %build_adjacency.2 = (f32[1024,2560]{1,0:T(8,128)}, f32[1024,128]{1,0:T(8,128)}, f32[1024,128]{1,0:T(8,128)}, s32[2]{0:T(128)}) custom-call(s32[1032]{0:T(1024)} %concatenate.33.kf_ref, s32[1032]{0:T(1024)} %concatenate.34.kl_ref, s32[2]{0:T(128)} %pad_add_fusion.1.begin_ref, s32[512,1,256]{2,1,0:T(1,128)} %bitcast.31, s32[512,1,256]{2,1,0:T(1,128)} %bitcast.35, ...), custom_call_target="tpu_custom_call" | custom-call | flops 16000000000 | bytes 20971520 | tf_op jit(solution)/shard_map/build_adjacency/pallas_call | solution.py:103
  75.5 2.1 collective-permute-done.2
  77.6 1.2 reduce-precision_convert_fusion.3
  78.8 1.2 fusion.5
  80.1 0.9 slice_add_fusion.2
  81.0 49.1 %build_adjacency.3 = (f32[2048,2560]{1,0:T(8,128)}, f32[2048,128]{1,0:T(8,128)}, f32[2048,128]{1,0:T(8,128)}, s32[2]{0:T(128)}) custom-call(s32[1032]{0:T(1024)} %concatenate.33.kf_ref, s32[1032]{0:T(1024)} %concatenate.34.kl_ref, s32[2]{0:T(128)} %get-tuple-element.29.begin_ref, s32[512,1,256]{2,1,0:T(1,128)} %bitcast.32, s32[512,1,256]{2,1,0:T(1,128)} %bitcast.36, ...), custom_call_target="tpu_custom_call" | custom-call | flops 32000000000 | bytes 41943040 | tf_op jit(solution)/shard_map/build_adjacency/pallas_call | solution.py:103
  130.0 5.0 %all-to-all-start.1 = ((f32[64,16,128]{2,1,0:T(8,128)}), f32[64,16,128]{2,1,0:T(8,128)S(1)}, u32[]{:S(2)}, u32[]{:S(2)}) async-start(f32[64,16,128]{2,1,0:T(8,128)} %bitcast.10), calls=%async_computation.1 | async-start | bytes 1048576 | tf_op jit(solution)/shard_map/all_to_all | solution.py:249
  135.1 0.4 collective-permute-start.5
  135.5 13.5 %all-to-all-done.1 = f32[64,16,128]{2,1,0:T(8,128)S(1)} async-done(((f32[64,16,128]{2,1,0:T(8,128)}), f32[64,16,128]{2,1,0:T(8,128)S(1)}, u32[]{:S(2)}, u32[]{:S(2)}) %all-to-all-start.1) | async-done | bytes 524320 | tf_op jit(solution)/shard_map/all_to_all | solution.py:249
  149.0 0.1 reduce_sum.38
  149.1 0.1 add_add_fusion.1
  149.2 1.1 scatter_fusion
  150.3 0.1 maximum_convert_fusion
  150.3 0.1 collective-permute-start.4
  150.5 0.4 fusion.43
  150.9 1.5 collective-permute-done.4
  152.3 0.4 fusion.8
  152.8 3.8 %fusion.10 = bf16[2048,256]{1,0:T(8,128)(2,1)} fusion(bf16[2048,256]{1,0:T(8,128)(2,1)S(1)} %fusion.8, s32[2048]{0:T(1024)S(1)} %eq.81), kind=kOutput, calls=%fused_computation.18 | convolution fusion | flops 2152202240 | bytes 2105344 | tf_op jit(solution)/shard_map/dot_general | solution.py:233
  156.6 4.7 %all-to-all-start.2 = ((bf16[64,32,256]{2,1,0:T(8,128)(2,1)}), bf16[64,32,256]{2,1,0:T(8,128)(2,1)S(1)}, u32[]{:S(2)}, u32[]{:S(2)}) async-start(bf16[64,32,256]{2,1,0:T(8,128)(2,1)} %bitcast.11), calls=%async_computation.2 | async-start | bytes 2097152 | tf_op jit(solution)/shard_map/all_to_all | solution.py:234
  161.4 19.3 %all-to-all-done.2 = bf16[64,32,256]{2,1,0:T(8,128)(2,1)S(1)} async-done(((bf16[64,32,256]{2,1,0:T(8,128)(2,1)}), bf16[64,32,256]{2,1,0:T(8,128)(2,1)S(1)}, u32[]{:S(2)}, u32[]{:S(2)}) %all-to-all-start.2) | async-done | bytes 1048608 | tf_op jit(solution)/shard_map/all_to_all | solution.py:234
  180.7 0.1 fusion.44
  180.8 0.5 fusion.16
  181.3 1.2 pad_maximum_fusion.1.refs_5_
  182.5 8.8 %multiply_adjacency.2 = (f32[1024,128]{1,0:T(8,128)}, f32[1024,128]{1,0:T(8,128)}) custom-call(f32[1024,2560]{1,0:T(8,128)} %get-tuple-element.31.refs_0_.refs_1_.refs_2_.refs_3_.refs_4_, f32[1024,2560]{1,0:T(8,128)} %get-tuple-element.31.refs_0_.refs_1_.refs_2_.refs_3_.refs_4_, f32[1024,2560]{1,0:T(8,128)} %get-tuple-element.31.refs_0_.refs_1_.refs_2_.refs_3_.refs_4_, ...), custom_call_target="tpu_custom_call" | custom-call | flops 4026531840 | bytes 10485760 | tf_op jit(solution)/shard_map/multiply_adjacency/pallas_call | solution.py:143
  191.3 2.1 collective-permute-done.6
  193.4 1.2 reduce-precision_convert_fusion.1
  194.6 1.2 fusion.4
  195.9 0.1 slice_add_fusion
  196.0 15.0 %multiply_adjacency.3 = (f32[2048,128]{1,0:T(8,128)}, f32[2048,128]{1,0:T(8,128)}) custom-call(f32[2048,2560]{1,0:T(8,128)} %get-tuple-element.30.refs_0_.refs_1_.refs_2_.refs_3_.refs_4_, f32[2048,2560]{1,0:T(8,128)} %get-tuple-element.30.refs_0_.refs_1_.refs_2_.refs_3_.refs_4_, f32[2048,2560]{1,0:T(8,128)} %get-tuple-element.30.refs_0_.refs_1_.refs_2_.refs_3_.refs_4_, ...), custom_call_target="tpu_custom_call" | custom-call | flops 8053063680 | bytes 20971520 | tf_op jit(solution)/shard_map/multiply_adjacency/pallas_call | solution.py:143
  211.0 0.2 collective-permute-start.7
  211.2 18.4 %all_to_all.20 = f32[64,16,128]{2,1,0:T(8,128)S(1)} all-to-all(f32[64,16,128]{2,1,0:T(8,128)S(1)} %bitcast.30), channel_id=1, replica_groups=mesh['data'=1,'feat'=2,'graph'=64] {'graph'}, dimensions={0} | all-to-all | bytes 1048576 | tf_op jit(solution)/shard_map/all_to_all | solution.py:249
  229.6 0.1 reduce_sum.39
  229.7 1.1 add_add_fusion
  230.8 2.8 %scatter_fusion.1 = f32[2048,128]{1,0:T(8,128)} fusion(f32[2048,128]{1,0:T(8,128)} %add_add_fusion, s32[16]{0:T(128)S(1)} %get-tuple-element.43, f32[16,128]{1,0:T(8,128)S(1)} %reduce_sum.39), kind=kCustom, calls=%fused_computation.1 | custom fusion | flops 2048 | bytes 24640 | tf_op jit(solution)/shard_map/scatter-add | solution.py:253
  (40 shorter events, 0.2 us)
Async XLA Ops:
  6.5 4.0 %copy-start.2 = (f32[102400]{0:T(1024)S(1)}, f32[102400]{0:T(1024)}, u32[]{:S(2)}) copy-start(f32[102400]{0:T(1024)} %param.16) | copy-start | bytes 1228804
  6.5 44.2 %sort.23.cloned.1.call-start = ((), (), s32[]{:S(2)}) async-start(), calls=%async_computation.4 | async-start | bytes 4718624 | tf_op jit(solution)/shard_map/sort | solution.py:205
  7.3 6.6 %collective-permute-start = (bf16[50,256]{1,0:T(8,128)(2,1)S(1)}, bf16[50,256]{1,0:T(8,128)(2,1)S(1)}, u32[]{:S(2)}, u32[]{:S(2)}) collective-permute-start(bf16[50,256]{1,0:T(8,128)(2,1)S(1)} %pad_maximum_fusion.3), channel_id=1, source_target_pairs={{0,64},{64,0},{1,65},{65,1},{2,66},{66,2},{3,67},{67,3},{4,68},{68... | collective-permute-start | bytes 76808 | tf_op jit(solution)/shard_map/ppermute | solution.py:179
  7.4 6.5 %collective-permute-start.1 = (bf16[2048,50]{0,1:T(8,128)(2,1)}, bf16[2048,50]{0,1:T(8,128)(2,1)S(1)}, u32[]{:S(2)}, u32[]{:S(2)}) collective-permute-start(bf16[2048,50]{0,1:T(8,128)(2,1)} %param.12), channel_id=1, source_target_pairs={{0,64},{64,0},{1,65},{65,1},{2,66},{66,2},{3,67},{67,3},{4,68},{68... | collective-permute-start | bytes 614408 | tf_op jit(solution)/shard_map/ppermute | solution.py:230
  9.7 2.6 %copy-start.3 = (bf16[2048,50]{0,1:T(8,128)(2,1)S(1)}, bf16[2048,50]{0,1:T(8,128)(2,1)}, u32[]{:S(2)}) copy-start(bf16[2048,50]{0,1:T(8,128)(2,1)} %param.12) | copy-start | bytes 614404
  12.2 0.7 copy-start.5
  12.2 1.5 copy-start.6
  12.2 1.5 copy-start.7
  18.3 30.7 %all-to-all-start = ((bf16[64,32,256]{2,1,0:T(8,128)(2,1)}), bf16[64,32,256]{2,1,0:T(8,128)(2,1)S(1)}, u32[]{:S(2)}, u32[]{:S(2)}) async-start(bf16[64,32,256]{2,1,0:T(8,128)(2,1)} %bitcast.5), calls=%async_computation | async-start | bytes 2097152 | tf_op jit(solution)/shard_map/all_to_all | solution.py:234
  75.5 2.1 collective-permute-start.2
  81.0 54.0 %copy-start.4 = (bf16[128,256]{1,0:T(8,128)(2,1)S(1)}, bf16[128,256]{1,0:T(8,128)(2,1)}, u32[]{:S(2)}) copy-start(bf16[128,256]{1,0:T(8,128)(2,1)} %param.21) | copy-start | bytes 196612
  81.0 68.1 %copy-start.8 = (f32[128]{0:T(128)S(1)}, f32[128]{0:T(128)}, u32[]{:S(2)}) copy-start(f32[128]{0:T(128)} %param.22) | copy-start | bytes 1540
  130.0 19.1 %copy-start = (f32[2048,128]{1,0:T(8,128)S(1)}, f32[2048,128]{1,0:T(8,128)}, u32[]{:S(2)}) copy-start(f32[2048,128]{1,0:T(8,128)} %get-tuple-element.32) | copy-start | bytes 3145732
  130.0 19.0 %collective-permute-start.3 = (f32[2048,128]{1,0:T(8,128)}, f32[2048,128]{1,0:T(8,128)S(1)}, u32[]{:S(2)}, u32[]{:S(2)}) collective-permute-start(f32[2048,128]{1,0:T(8,128)} %get-tuple-element.33), channel_id=1, source_target_pairs={{0,64},{64,0},{1,65},{65,1},{2,66},{66,2},{3,67},{67,3},{4,68},{68... | collective-permute-start | bytes 3145736 | tf_op jit(solution)/shard_map/ppermute | solution.py:253
  130.0 19.0 %all-to-all-start.1 = ((f32[64,16,128]{2,1,0:T(8,128)}), f32[64,16,128]{2,1,0:T(8,128)S(1)}, u32[]{:S(2)}, u32[]{:S(2)}) async-start(f32[64,16,128]{2,1,0:T(8,128)} %bitcast.10), calls=%async_computation.1 | async-start | bytes 1048576 | tf_op jit(solution)/shard_map/all_to_all | solution.py:249
  135.1 15.4 %collective-permute-start.5 = (bf16[128,256]{1,0:T(8,128)(2,1)S(1)}, bf16[128,256]{1,0:T(8,128)(2,1)S(1)}, u32[]{:S(2)}, u32[]{:S(2)}) collective-permute-start(bf16[128,256]{1,0:T(8,128)(2,1)S(1)} %pad_maximum_fusion.2), channel_id=1, source_target_pairs={{0,64},{64,0},{1,65},{65,1},{2,66},{66,2},{3,67},{67,3},{4,68},{68... | collective-permute-start | bytes 196616 | tf_op jit(solution)/shard_map/ppermute | solution.py:179
  150.3 2.0 collective-permute-start.4
  156.6 24.1 %all-to-all-start.2 = ((bf16[64,32,256]{2,1,0:T(8,128)(2,1)}), bf16[64,32,256]{2,1,0:T(8,128)(2,1)S(1)}, u32[]{:S(2)}, u32[]{:S(2)}) async-start(bf16[64,32,256]{2,1,0:T(8,128)(2,1)} %bitcast.11), calls=%async_computation.2 | async-start | bytes 2097152 | tf_op jit(solution)/shard_map/all_to_all | solution.py:234
  191.3 2.1 collective-permute-start.6
  196.0 33.7 %copy-start.9 = (f32[128]{0:T(128)S(1)}, f32[128]{0:T(128)}, u32[]{:S(2)}) copy-start(f32[128]{0:T(128)} %param.23) | copy-start | bytes 1540
  211.0 18.7 %copy-start.1 = (f32[2048,128]{1,0:T(8,128)S(1)}, f32[2048,128]{1,0:T(8,128)}, u32[]{:S(2)}) copy-start(f32[2048,128]{1,0:T(8,128)} %get-tuple-element.38) | copy-start | bytes 3145732
  211.0 18.7 %collective-permute-start.7 = (f32[2048,128]{1,0:T(8,128)}, f32[2048,128]{1,0:T(8,128)S(1)}, u32[]{:S(2)}, u32[]{:S(2)}) collective-permute-start(f32[2048,128]{1,0:T(8,128)} %get-tuple-element.39), channel_id=1, source_target_pairs={{0,64},{64,0},{1,65},{65,1},{2,66},{66,2},{3,67},{67,3},{4,68},{68... | collective-permute-start | bytes 3145736 | tf_op jit(solution)/shard_map/ppermute | solution.py:253
Sparse Core Ops, SparseCore 0:
  12.4 24.4 sort.25.cloned.1.call-done
  (1 shorter events, 0.0 us)
where the time goes:
time: 243 us; the launch traced here: 240 us
  Pallas kernels  93.3 us (38%)
  waiting for transfers between devices  57.6 us (24%)
  starting transfers between devices  22.5 us (9%)
  blocking collectives  18.4 us (8%)
  other arithmetic  16.1 us (7%)
  between operations  13.7 us (6%)
  matrix products  13 us (5%)
  local copies, waits for them, and re-layouts  5.79 us (2%)
    pallas_call x2, Pallas kernels, build_and_multiply(): pl.pallas_call(functools.partial(build_kernel, n_src, first_block), grid_...  69.5 us
    all_to_all x2, waiting for transfers between devices, table_of(): lax.all_to_all(out.reshape(n_graph, s_half + own_hubs, 2 * width), 'graph...  38.4 us
    pallas_call x2, Pallas kernels, multiply(): pl.pallas_call(multiply_kernel, grid=(rows // tall,), in_specs=[strip(j)...  23.8 us
    all_to_all x1, blocking collectives, hub_total(): lax.all_to_all(parts.reshape(n_graph, own_hubs, width), 'graph', 0, 0, ti...  18.4 us
    all_to_all x2, starting transfers between devices, table_of(): lax.all_to_all(out.reshape(n_graph, s_half + own_hubs, 2 * width), 'graph...  16.2 us
    all_to_all x1, waiting for transfers between devices, hub_total(): lax.all_to_all(parts.reshape(n_graph, own_hubs, width), 'graph', 0, 0, ti...  13.5 us
    dot_general x2, matrix products, table_of(): out = jnp.dot(send_hot, z, preferred_element_type=F32).astype(BF)  7.66 us
    all_to_all x1, starting transfers between devices, hub_total(): lax.all_to_all(parts.reshape(n_graph, own_hubs, width), 'graph', 0, 0, ti...  4.96 us
  transfers between devices with their start and end apart: 11, of which 6 were waited for; matrix products, arithmetic and copies ran while one was open for 3% of the time, Pallas kernels for 0%

commit v1 on v0

--- a/solution.py
+++ b/solution.py
@@ -15,7 +15,7 @@
 UNROLL = 8
 BF = jnp.bfloat16
 F32 = jnp.float32
-VMEM_LIMIT = 56 << 20
+VMEM_LIMIT = 60 << 20
 
 
 def over(a, n):
@@ -30,127 +30,139 @@
     return hi, mid, low
 
 
-def product(load, table_ref):
+def product(a_ref, start, table_ref):
     depth, _ = table_ref.shape
     total = None
     for k in range(0, depth, SB):
-        pieces = jnp.concatenate(split3(load(k)), axis=0)
+        pieces = jnp.concatenate(split3(a_ref[pl.ds(start, DB), k : k + SB]), axis=0)
         part = jnp.dot(pieces, table_ref[k : k + SB, :], preferred_element_type=F32)
         total = part if total is None else total + part
-    rows = total.shape[0] // 3
-    return total[:rows] + total[rows : 2 * rows] + total[2 * rows :]
-
-
-def store_halves(y, mine_ref, other_ref):
+    return total[:DB] + total[DB : 2 * DB] + total[2 * DB :]
+
+
+def write_product(a_ref, i, table_ref, mine_ref, other_ref):
     width = mine_ref.shape[1]
-    mine_ref[...] = y[:, :width]
-    other_ref[...] = y[:, width:]
-
-
-def build_kernel(n_src, first_block, kf_ref, kl_ref, begin_ref, key_ref, low_ref, w_ref, table_ref, a_ref, mine_ref, other_ref, state_ref):
-    step = pl.program_id(0)
-    n_chunks = key_ref.shape[0]
-    per = CH // LANES
-
-    @pl.when(step == 0)
-    def _():
-        state_ref[0] = begin_ref[0]
-        state_ref[1] = begin_ref[1]
-
-    first = (first_block + step) * n_src
-    limit = first + n_src
-    a_ref[...] = jnp.zeros_like(a_ref)
+    start = pl.multiple_of(i * DB, DB)
+    y = product(a_ref, start, table_ref)
+    mine_ref[pl.ds(start, DB), :] = y[:, :width]
+    other_ref[pl.ds(start, DB), :] = y[:, width:]
+
+
+def block_copy(src, dst, i, sem):
+    rows = pl.ds(pl.multiple_of(i * DB, DB), DB)
+    return pltpu.make_async_copy(src.at[rows, :], dst.at[rows, :], sem.at[i])
+
+
+def multiply_kernel(a_hbm, table_ref, mine_ref, other_ref, a_ref, sem):
+    n_blocks = a_ref.shape[0] // DB
+
+    @pl.loop(0, n_blocks)
+    def _(i):
+        block_copy(a_hbm, a_ref, i, sem).start()
+
+    @pl.loop(0, n_blocks)
+    def _(i):
+        block_copy(a_hbm, a_ref, i, sem).wait()
+        write_product(a_ref, i, table_ref, mine_ref, other_ref)
+
+
+def build_kernel(first_block, kf_ref, kl_ref, begin_ref, key_ref, low_ref, w_ref, table_ref, a_hbm, mine_ref, other_ref, state_ref, a_ref, sem):
+    n_src = a_ref.shape[1] // SB
+    n_rows = key_ref.shape[0]
+    n_blocks = a_ref.shape[0] // DB
+    first = first_block * n_src
+    limit = first + n_blocks * n_src
+
+    @pl.loop(0, n_blocks)
+    def _(i):
+        a_ref[pl.ds(pl.multiple_of(i * DB, DB), DB), :] = jnp.zeros((DB, a_ref.shape[1]), F32)
+
+    def pair(ref, at):
+        return jnp.concatenate([ref[at], ref[at + 1]], axis=1)
 
     def body(carry):
-        chunk, bucket = carry
+        at, bucket = carry
         for _ in range(UNROLL):
             live = bucket < limit
-            here = jnp.minimum(chunk, n_chunks - 1)
-            lows = low_ref[here]
-            match = key_ref[here] == jnp.where(live, bucket, -1)
+            here = jnp.minimum(at, n_rows - 2)
+            lows = pair(low_ref, here)
+            match = pair(key_ref, here) == jnp.where(live, bucket, -1)
             d_low = jnp.where(match, lax.shift_right_logical(lows, 8), -1)
             s_low = lows & (SB - 1)
             d_mask = lax.broadcasted_iota(jnp.int32, (DB, CH), 0) == d_low
-            pieces = [jnp.where(d_mask, piece.astype(F32), 0.0).astype(BF) for piece in split3(w_ref[here])]
+            pieces = [jnp.where(d_mask, piece.astype(F32), 0.0).astype(BF) for piece in split3(pair(w_ref, here))]
             s_hot = jnp.where(lax.broadcasted_iota(jnp.int32, (SB, CH), 0) == s_low, 1.0, 0.0).astype(BF)
             got = lax.dot_general(
                 jnp.concatenate(pieces, axis=0), s_hot, (((1,), (1,)), ((), ())), preferred_element_type=F32
             )
             got = got[:DB] + got[DB : 2 * DB] + got[2 * DB :]
-            column = pl.multiple_of(jnp.clip(bucket - first, 0, n_src - 1) * SB, SB)
-            a_ref[:, pl.ds(column, SB)] += got
-            done = bucket >= kl_ref[here * per + per - 1]
-            next_chunk = chunk + jnp.where(done, 1, 0)
-            next_bucket = jnp.where(done, kf_ref[next_chunk * per], bucket + 1)
-            chunk = jnp.where(live, next_chunk, chunk)
+            place = jnp.clip(bucket - first, 0, n_blocks * n_src - 1)
+            block = place // n_src
+            column = pl.multiple_of((place - block * n_src) * SB, SB)
+            a_ref[pl.ds(pl.multiple_of(block * DB, DB), DB), pl.ds(column, SB)] += got
+            more = kl_ref[here + 1] == bucket
+            next_at = here + jnp.where(more, 2, jnp.where(kl_ref[here] <= bucket, 1, 0))
+            next_bucket = jnp.maximum(kf_ref[next_at], jnp.where(more, bucket, bucket + 1))
+            at = jnp.where(live, next_at, at)
             bucket = jnp.where(live, next_bucket, bucket)
-        return chunk, bucket
-
-    chunk, bucket = lax.while_loop(lambda c: c[1] < limit, body, (state_ref[0], state_ref[1]))
-    state_ref[0] = chunk
+        return at, bucket
+
+    at, bucket = lax.while_loop(lambda c: c[1] < limit, body, (begin_ref[0], begin_ref[1]))
+    state_ref[0] = at
     state_ref[1] = bucket
-    store_halves(product(lambda k: a_ref[:, k : k + SB], table_ref), mine_ref, other_ref)
+
+    @pl.loop(0, n_blocks)
+    def _(i):
+        block_copy(a_ref, a_hbm, i, sem).start()
+
+    @pl.loop(0, n_blocks)
+    def _(i):
+        write_product(a_ref, i, table_ref, mine_ref, other_ref)
+
+    @pl.loop(0, n_blocks)
+    def _(i):
+        block_copy(a_ref, a_hbm, i, sem).wait()
+
+
+HBM_SPEC = pl.BlockSpec(memory_space=pltpu.HBM)
+SMEM_SPEC = pl.BlockSpec(memory_space=pltpu.SMEM)
+VMEM_SPEC = pl.BlockSpec(memory_space=pltpu.VMEM)
 
 
 def build_and_multiply(edges, begin, table, first_block, n_blocks):
     k_first, k_last, keys, low, w = edges
     depth, full = table.shape
-    n_src = depth // SB
-    n_chunks = keys.shape[0]
-    whole = lambda *shape: pl.BlockSpec(shape, lambda i, *_: (0,) * len(shape), pipeline_mode=pl.Buffered(1))
     rows = n_blocks * DB
-    half = pl.BlockSpec((DB, full // 2), lambda i, *_: (i, 0))
     return pl.pallas_call(
-        functools.partial(build_kernel, n_src, first_block),
-        grid_spec=pltpu.PrefetchScalarGridSpec(
-            num_scalar_prefetch=3,
-            grid=(n_blocks,),
-            in_specs=[whole(n_chunks, 1, CH)] * 3 + [whole(depth, full)],
-            out_specs=[
-                pl.BlockSpec((DB, depth), lambda i, *_: (i, 0)),
-                half,
-                half,
-                pl.BlockSpec(memory_space=pltpu.SMEM),
-            ],
-        ),
+        functools.partial(build_kernel, first_block),
+        in_specs=[SMEM_SPEC] * 3 + [VMEM_SPEC] * 4,
+        out_specs=[HBM_SPEC, VMEM_SPEC, VMEM_SPEC, SMEM_SPEC],
+        scratch_shapes=[pltpu.VMEM((rows, depth), F32), pltpu.SemaphoreType.DMA((n_blocks,))],
         out_shape=[
             jax.ShapeDtypeStruct((rows, depth), F32),
             jax.ShapeDtypeStruct((rows, full // 2), F32),
             jax.ShapeDtypeStruct((rows, full // 2), F32),
             jax.ShapeDtypeStruct((2,), jnp.int32),
         ],
-        compiler_params=pltpu.CompilerParams(dimension_semantics=("arbitrary",), vmem_limit_bytes=VMEM_LIMIT),
-        cost_estimate=pl.CostEstimate(flops=n_blocks * 2 * 10**9, bytes_accessed=8 * rows * depth, transcendentals=0),
+        compiler_params=pltpu.CompilerParams(vmem_limit_bytes=VMEM_LIMIT),
+        cost_estimate=pl.CostEstimate(flops=n_blocks * 2 * 10**9, bytes_accessed=10**7, transcendentals=0),
         name="build_adjacency",
     )(k_first, k_last, begin, keys, low, w, table)
-
-
-def multiply_kernel(*refs):
-    *a_refs, table_ref, mine_ref, other_ref = refs
-    cols = a_refs[0].shape[1]
-    load = lambda k: a_refs[k // cols][:, k % cols : k % cols + SB]
-    store_halves(product(load, table_ref), mine_ref, other_ref)
 
 
 def multiply(a, table):
     rows, depth = a.shape
     full = table.shape[1]
-    cols = 2 * SB
-    tall = 2 * DB
-    half = pl.BlockSpec((tall, full // 2), lambda i: (i, 0))
-    strip = lambda j: pl.BlockSpec((tall, cols), lambda i: (i, j))
-    n_strips = depth // cols
     return pl.pallas_call(
         multiply_kernel,
-        grid=(rows // tall,),
-        in_specs=[strip(j) for j in range(n_strips)]
-        + [pl.BlockSpec((depth, full), lambda i: (0, 0), pipeline_mode=pl.Buffered(1))],
-        out_specs=[half, half],
+        in_specs=[HBM_SPEC, VMEM_SPEC],
+        out_specs=[VMEM_SPEC] * 2,
+        scratch_shapes=[pltpu.VMEM((rows, depth), F32), pltpu.SemaphoreType.DMA((rows // DB,))],
         out_shape=[jax.ShapeDtypeStruct((rows, full // 2), F32)] * 2,
-        compiler_params=pltpu.CompilerParams(dimension_semantics=("arbitrary",), vmem_limit_bytes=VMEM_LIMIT),
-        cost_estimate=pl.CostEstimate(flops=6 * rows * depth * full, bytes_accessed=4 * rows * depth, transcendentals=0),
+        compiler_params=pltpu.CompilerParams(vmem_limit_bytes=VMEM_LIMIT),
+        cost_estimate=pl.CostEstimate(flops=6 * rows * depth * full, bytes_accessed=10**7, transcendentals=0),
         name="multiply_adjacency",
-    )(*[a] * n_strips, table)
+    )(a, table)
 
 
 def solution(mesh):
@@ -198,7 +210,7 @@
         target = jnp.where(dst >= verts, dst - verts, dst + hubs)
         bucket = lax.shift_right_logical(target, 7) * n_src + lax.shift_right_logical(row, 8)
         n_edges = dst.shape[0]
-        padded = -(-max(n_edges, 131072) // CH) * CH
+        padded = -(-max(n_edges + 2 * CH, 131072) // CH) * CH
         fill = (0, padded - n_edges)
         key = jnp.pad(jnp.where((valid > 0) & (half == col), bucket, none), fill, constant_values=none)
         low = jnp.pad((target & (DB - 1)) * SB + (row & (SB - 1)), fill)
@@ -207,8 +219,8 @@
         end = jnp.full((8,), none, jnp.int32)
         k_first = jnp.concatenate([jnp.min(key_rows, axis=1), end])
         k_last = jnp.concatenate([jnp.max(key_rows, axis=1), end])
-        chunks = lambda a: a.reshape(padded // CH, 1, CH)
-        edges = (k_first, k_last, chunks(key), chunks(low), chunks(w_sorted))
+        rows_of = lambda a: a.reshape(-1, 1, LANES)
+        edges = (k_first, k_last, rows_of(key), rows_of(low), rows_of(w_sorted))
 
         owner = over(hub_ids, verts)
         ids = jnp.arange(hubs)

time: 243 us -> 230 us (0.947)
  Pallas kernels: 93.3 us -> 80.5 us
    pallas_call x4, Pallas kernels: 93.3 us -> 80.5 us  [the longest x2 56.4 us: build_and_multiply(): pl.pallas_call(functools.partial(build_kernel, first_block), in_specs=[SM...]
where the time goes in v1:
time: 230 us; the launch traced here: 228 us
  Pallas kernels  80.5 us (35%)
  waiting for transfers between devices  57.7 us (25%)
  starting transfers between devices  22.8 us (10%)
  blocking collectives  18.4 us (8%)
  other arithmetic  16.1 us (7%)
  between operations  13.8 us (6%)
  matrix products  13 us (6%)
  local copies, waits for them, and re-layouts  5.8 us (3%)
    pallas_call x2, Pallas kernels, build_and_multiply(): pl.pallas_call(functools.partial(build_kernel, first_block), in_specs=[SM...  56.4 us
    all_to_all x2, waiting for transfers between devices, table_of(): lax.all_to_all(out.reshape(n_graph, s_half + own_hubs, 2 * width), 'graph...  38.4 us
    pallas_call x2, Pallas kernels, multiply(): pl.pallas_call(multiply_kernel, in_specs=[HBM_SPEC, VMEM_SPEC], out_specs...  24.1 us
    all_to_all x1, blocking collectives, hub_total(): lax.all_to_all(parts.reshape(n_graph, own_hubs, width), 'graph', 0, 0, ti...  18.4 us
    all_to_all x2, starting transfers between devices, table_of(): lax.all_to_all(out.reshape(n_graph, s_half + own_hubs, 2 * width), 'graph...  16.2 us
    all_to_all x1, waiting for transfers between devices, hub_total(): lax.all_to_all(parts.reshape(n_graph, own_hubs, width), 'graph', 0, 0, ti...  13.7 us
    dot_general x2, matrix products, table_of(): out = jnp.dot(send_hot, z, preferred_element_type=F32).astype(BF)  7.66 us
    all_to_all x1, starting transfers between devices, hub_total(): lax.all_to_all(parts.reshape(n_graph, own_hubs, width), 'graph', 0, 0, ti...  4.96 us
  transfers between devices with their start and end apart: 11, of which 6 were waited for; matrix products, arithmetic and copies ran while one was open for 3% of the time, Pallas kernels for 0%

profile of v1, /device:TPU:0, one launch (start us, length us, event | category | flops | bytes accessed | tf_op | source)
XLA Modules:
  0.0 228.1 jit_solution(8868187548954681357)
XLA Ops:
  6.5 0.8 constant_dynamic-slice_fusion.4
  7.3 0.1 collective-permute-start
  7.4 0.5 collective-permute-start.1
  7.9 1.7 and_add_fusion
  9.7 0.8 pad.14
  10.5 0.8 pad.15
  11.3 0.9 pad.13
  12.2 0.5 fusion.42
  12.7 0.1 copy-done.5
  12.9 0.5 convert_reduce_fusion
  13.4 0.2 select_reduce_fusion
  13.6 0.1 pad.33.clone
  13.7 0.1 pad_add_fusion
  13.8 0.1 copy.20
  13.9 0.1 eq.81
  14.0 0.5 fusion.7
  14.5 3.8 %fusion.9 = bf16[2048,256]{1,0:T(8,128)(2,1)} fusion(bf16[256,2048]{0,1:T(8,128)(2,1)S(1)} %fusion.7, s32[2048]{0:T(1024)S(1)} %eq.81), kind=kOutput, calls=%fused_computation.17 | convolution fusion | flops 2152202240 | bytes 2105344 | tf_op jit(solution)/shard_map/dot_general | solution.py:245
  18.3 11.5 %all-to-all-start = ((bf16[64,32,256]{2,1,0:T(8,128)(2,1)}), bf16[64,32,256]{2,1,0:T(8,128)(2,1)S(1)}, u32[]{:S(2)}, u32[]{:S(2)}) async-start(bf16[64,32,256]{2,1,0:T(8,128)(2,1)} %bitcast.5), calls=%async_computation | async-start | bytes 2097152 | tf_op jit(solution)/shard_map/all_to_all | solution.py:246
  29.8 0.1 dynamic_slice.28
  29.9 19.0 %all-to-all-done = bf16[64,32,256]{2,1,0:T(8,128)(2,1)S(1)} async-done(((bf16[64,32,256]{2,1,0:T(8,128)(2,1)}), bf16[64,32,256]{2,1,0:T(8,128)(2,1)S(1)}, u32[]{:S(2)}, u32[]{:S(2)}) %all-to-all-start) | async-done | bytes 1048608 | tf_op jit(solution)/shard_map/all_to_all | solution.py:246
  49.0 0.1 fusion.45
  49.1 0.5 fusion.15
  49.6 1.2 pad_maximum_fusion.table_ref
  50.8 1.4 bitcast_reduce_fusion
  52.1 0.5 slice.45
  52.7 0.6 concatenate.33.kf_ref
  53.3 0.6 concatenate.34.kl_ref
  53.9 1.2 pad_add_fusion.1.begin_ref
  55.1 15.6 %build_adjacency.2 = (f32[1024,2560]{1,0:T(8,128)}, f32[1024,128]{1,0:T(8,128)}, f32[1024,128]{1,0:T(8,128)}, s32[2]{0:T(128)}) custom-call(s32[1032]{0:T(1024)} %concatenate.33.kf_ref, s32[1032]{0:T(1024)} %concatenate.34.kl_ref, s32[2]{0:T(128)} %pad_add_fusion.1.begin_ref, s32[1024,1,128]{2,1,0:T(1,128)} %bitcast.31, s32[1024,1,128]{2,1,0:T(1,128)} %bitcast.35, ...), custom_call_target="tpu_custom_call" | custom-call | flops 16000000000 | bytes 10000000 | tf_op jit(solution)/shard_map/build_adjacency/pallas_call | solution.py:136
  70.7 0.1 collective-permute-start.2
  70.8 2.1 collective-permute-done.2
  72.9 1.2 reduce-precision_convert_fusion.3
  74.1 1.2 fusion.5
  75.3 0.9 slice_add_fusion.2
  76.2 40.8 %build_adjacency.3 = (f32[2048,2560]{1,0:T(8,128)}, f32[2048,128]{1,0:T(8,128)}, f32[2048,128]{1,0:T(8,128)}, s32[2]{0:T(128)}) custom-call(s32[1032]{0:T(1024)} %concatenate.33.kf_ref, s32[1032]{0:T(1024)} %concatenate.34.kl_ref, s32[2]{0:T(128)} %get-tuple-element.29.begin_ref, s32[1024,1,128]{2,1,0:T(1,128)} %bitcast.32, s32[1024,1,128]{2,1,0:T(1,128)} %bitcast.36, ...), custom_call_target="tpu_custom_call" | custom-call | flops 32000000000 | bytes 10000000 | tf_op jit(solution)/shard_map/build_adjacency/pallas_call | solution.py:136
  117.0 0.1 collective-permute-start.3
  117.1 5.0 %all-to-all-start.1 = ((f32[64,16,128]{2,1,0:T(8,128)}), f32[64,16,128]{2,1,0:T(8,128)S(1)}, u32[]{:S(2)}, u32[]{:S(2)}) async-start(f32[64,16,128]{2,1,0:T(8,128)} %bitcast.10), calls=%async_computation.1 | async-start | bytes 1048576 | tf_op jit(solution)/shard_map/all_to_all | solution.py:261
  122.2 0.4 collective-permute-start.5
  122.6 13.7 %all-to-all-done.1 = f32[64,16,128]{2,1,0:T(8,128)S(1)} async-done(((f32[64,16,128]{2,1,0:T(8,128)}), f32[64,16,128]{2,1,0:T(8,128)S(1)}, u32[]{:S(2)}, u32[]{:S(2)}) %all-to-all-start.1) | async-done | bytes 524320 | tf_op jit(solution)/shard_map/all_to_all | solution.py:261
  136.3 0.1 reduce_sum.38
  136.4 0.1 add_add_fusion.1
  136.5 1.1 scatter_fusion
  137.6 0.1 collective-permute-start.4
  137.7 0.4 fusion.43
  138.2 1.5 collective-permute-done.4
  139.6 0.4 fusion.8
  140.0 3.8 %fusion.10 = bf16[2048,256]{1,0:T(8,128)(2,1)} fusion(bf16[2048,256]{1,0:T(8,128)(2,1)S(1)} %fusion.8, s32[2048]{0:T(1024)S(1)} %eq.81), kind=kOutput, calls=%fused_computation.18 | convolution fusion | flops 2152202240 | bytes 2105344 | tf_op jit(solution)/shard_map/dot_general | solution.py:245
  143.9 4.7 %all-to-all-start.2 = ((bf16[64,32,256]{2,1,0:T(8,128)(2,1)}), bf16[64,32,256]{2,1,0:T(8,128)(2,1)S(1)}, u32[]{:S(2)}, u32[]{:S(2)}) async-start(bf16[64,32,256]{2,1,0:T(8,128)(2,1)} %bitcast.11), calls=%async_computation.2 | async-start | bytes 2097152 | tf_op jit(solution)/shard_map/all_to_all | solution.py:246
  148.6 19.3 %all-to-all-done.2 = bf16[64,32,256]{2,1,0:T(8,128)(2,1)S(1)} async-done(((bf16[64,32,256]{2,1,0:T(8,128)(2,1)}), bf16[64,32,256]{2,1,0:T(8,128)(2,1)S(1)}, u32[]{:S(2)}, u32[]{:S(2)}) %all-to-all-start.2) | async-done | bytes 1048608 | tf_op jit(solution)/shard_map/all_to_all | solution.py:246
  168.0 0.1 fusion.44
  168.1 0.5 fusion.16
  168.6 1.2 pad_maximum_fusion.1.table_ref
  169.8 9.1 %multiply_adjacency.2 = (f32[1024,128]{1,0:T(8,128)}, f32[1024,128]{1,0:T(8,128)}) custom-call(f32[1024,2560]{1,0:T(8,128)} %get-tuple-element.31.a_hbm, bf16[2560,256]{1,0:T(8,128)(2,1)} %pad_maximum_fusion.1.table_ref), custom_call_target="tpu_custom_call" | custom-call | flops 4026531840 | bytes 10000000 | tf_op jit(solution)/shard_map/multiply_adjacency/pallas_call | solution.py:156
  178.9 0.1 collective-permute-start.6
  179.0 2.1 collective-permute-done.6
  181.1 1.2 reduce-precision_convert_fusion.1
  182.3 1.3 fusion.4
  183.6 0.1 slice_add_fusion
  183.6 14.9 %multiply_adjacency.3 = (f32[2048,128]{1,0:T(8,128)}, f32[2048,128]{1,0:T(8,128)}) custom-call(f32[2048,2560]{1,0:T(8,128)} %get-tuple-element.30.a_hbm, bf16[2560,256]{1,0:T(8,128)(2,1)} %pad_maximum_fusion.1.table_ref), custom_call_target="tpu_custom_call" | custom-call | flops 8053063680 | bytes 10000000 | tf_op jit(solution)/shard_map/multiply_adjacency/pallas_call | solution.py:156
  198.6 0.2 collective-permute-start.7
  198.8 18.4 %all_to_all.20 = f32[64,16,128]{2,1,0:T(8,128)S(1)} all-to-all(f32[64,16,128]{2,1,0:T(8,128)S(1)} %bitcast.30), channel_id=1, replica_groups=mesh['data'=1,'feat'=2,'graph'=64] {'graph'}, dimensions={0} | all-to-all | bytes 1048576 | tf_op jit(solution)/shard_map/all_to_all | solution.py:261
  217.2 0.1 reduce_sum.39
  217.3 1.1 add_add_fusion
  218.4 2.8 %scatter_fusion.1 = f32[2048,128]{1,0:T(8,128)} fusion(f32[2048,128]{1,0:T(8,128)} %add_add_fusion, s32[16]{0:T(128)S(1)} %get-tuple-element.43, f32[16,128]{1,0:T(8,128)S(1)} %reduce_sum.39), kind=kCustom, calls=%fused_computation.1 | custom fusion | flops 2048 | bytes 24640 | tf_op jit(solution)/shard_map/scatter-add | solution.py:265
  (40 shorter events, 0.3 us)
Async XLA Ops:
  6.5 4.0 %copy-start.2 = (f32[102400]{0:T(1024)S(1)}, f32[102400]{0:T(1024)}, u32[]{:S(2)}) copy-start(f32[102400]{0:T(1024)} %param.16) | copy-start | bytes 1228804
  6.5 44.2 %sort.23.cloned.1.call-start = ((), (), s32[]{:S(2)}) async-start(), calls=%async_computation.4 | async-start | bytes 4718624 | tf_op jit(solution)/shard_map/sort | solution.py:217
  7.3 6.6 %collective-permute-start = (bf16[50,256]{1,0:T(8,128)(2,1)S(1)}, bf16[50,256]{1,0:T(8,128)(2,1)S(1)}, u32[]{:S(2)}, u32[]{:S(2)}) collective-permute-start(bf16[50,256]{1,0:T(8,128)(2,1)S(1)} %pad_maximum_fusion.3), channel_id=1, source_target_pairs={{0,64},{64,0},{1,65},{65,1},{2,66},{66,2},{3,67},{67,3},{4,68},{68... | collective-permute-start | bytes 76808 | tf_op jit(solution)/shard_map/ppermute | solution.py:191
  7.4 6.5 %collective-permute-start.1 = (bf16[2048,50]{0,1:T(8,128)(2,1)}, bf16[2048,50]{0,1:T(8,128)(2,1)S(1)}, u32[]{:S(2)}, u32[]{:S(2)}) collective-permute-start(bf16[2048,50]{0,1:T(8,128)(2,1)} %param.12), channel_id=1, source_target_pairs={{0,64},{64,0},{1,65},{65,1},{2,66},{66,2},{3,67},{67,3},{4,68},{68... | collective-permute-start | bytes 614408 | tf_op jit(solution)/shard_map/ppermute | solution.py:242
  9.7 2.6 %copy-start.3 = (bf16[2048,50]{0,1:T(8,128)(2,1)S(1)}, bf16[2048,50]{0,1:T(8,128)(2,1)}, u32[]{:S(2)}) copy-start(bf16[2048,50]{0,1:T(8,128)(2,1)} %param.12) | copy-start | bytes 614404
  12.2 0.7 copy-start.5
  12.2 1.5 copy-start.6
  12.2 1.5 copy-start.7
  18.3 30.7 %all-to-all-start = ((bf16[64,32,256]{2,1,0:T(8,128)(2,1)}), bf16[64,32,256]{2,1,0:T(8,128)(2,1)S(1)}, u32[]{:S(2)}, u32[]{:S(2)}) async-start(bf16[64,32,256]{2,1,0:T(8,128)(2,1)} %bitcast.5), calls=%async_computation | async-start | bytes 2097152 | tf_op jit(solution)/shard_map/all_to_all | solution.py:246
  70.7 2.2 collective-permute-start.2
  76.2 45.9 %copy-start.4 = (bf16[128,256]{1,0:T(8,128)(2,1)S(1)}, bf16[128,256]{1,0:T(8,128)(2,1)}, u32[]{:S(2)}) copy-start(bf16[128,256]{1,0:T(8,128)(2,1)} %param.21) | copy-start | bytes 196612
  76.2 60.1 %copy-start.8 = (f32[128]{0:T(128)S(1)}, f32[128]{0:T(128)}, u32[]{:S(2)}) copy-start(f32[128]{0:T(128)} %param.22) | copy-start | bytes 1540
  117.0 19.3 %copy-start = (f32[2048,128]{1,0:T(8,128)S(1)}, f32[2048,128]{1,0:T(8,128)}, u32[]{:S(2)}) copy-start(f32[2048,128]{1,0:T(8,128)} %get-tuple-element.32) | copy-start | bytes 3145732
  117.0 19.3 %collective-permute-start.3 = (f32[2048,128]{1,0:T(8,128)}, f32[2048,128]{1,0:T(8,128)S(1)}, u32[]{:S(2)}, u32[]{:S(2)}) collective-permute-start(f32[2048,128]{1,0:T(8,128)} %get-tuple-element.33), channel_id=1, source_target_pairs={{0,64},{64,0},{1,65},{65,1},{2,66},{66,2},{3,67},{67,3},{4,68},{68... | collective-permute-start | bytes 3145736 | tf_op jit(solution)/shard_map/ppermute | solution.py:265
  117.1 19.1 %all-to-all-start.1 = ((f32[64,16,128]{2,1,0:T(8,128)}), f32[64,16,128]{2,1,0:T(8,128)S(1)}, u32[]{:S(2)}, u32[]{:S(2)}) async-start(f32[64,16,128]{2,1,0:T(8,128)} %bitcast.10), calls=%async_computation.1 | async-start | bytes 1048576 | tf_op jit(solution)/shard_map/all_to_all | solution.py:261
  122.2 15.6 %collective-permute-start.5 = (bf16[128,256]{1,0:T(8,128)(2,1)S(1)}, bf16[128,256]{1,0:T(8,128)(2,1)S(1)}, u32[]{:S(2)}, u32[]{:S(2)}) collective-permute-start(bf16[128,256]{1,0:T(8,128)(2,1)S(1)} %pad_maximum_fusion.2), channel_id=1, source_target_pairs={{0,64},{64,0},{1,65},{65,1},{2,66},{66,2},{3,67},{67,3},{4,68},{68... | collective-permute-start | bytes 196616 | tf_op jit(solution)/shard_map/ppermute | solution.py:191
  137.6 2.0 collective-permute-start.4
  143.9 24.1 %all-to-all-start.2 = ((bf16[64,32,256]{2,1,0:T(8,128)(2,1)}), bf16[64,32,256]{2,1,0:T(8,128)(2,1)S(1)}, u32[]{:S(2)}, u32[]{:S(2)}) async-start(bf16[64,32,256]{2,1,0:T(8,128)(2,1)} %bitcast.11), calls=%async_computation.2 | async-start | bytes 2097152 | tf_op jit(solution)/shard_map/all_to_all | solution.py:246
  178.9 2.2 collective-permute-start.6
  183.6 33.7 %copy-start.9 = (f32[128]{0:T(128)S(1)}, f32[128]{0:T(128)}, u32[]{:S(2)}) copy-start(f32[128]{0:T(128)} %param.23) | copy-start | bytes 1540
  198.6 18.7 %copy-start.1 = (f32[2048,128]{1,0:T(8,128)S(1)}, f32[2048,128]{1,0:T(8,128)}, u32[]{:S(2)}) copy-start(f32[2048,128]{1,0:T(8,128)} %get-tuple-element.38) | copy-start | bytes 3145732
  198.6 18.7 %collective-permute-start.7 = (f32[2048,128]{1,0:T(8,128)}, f32[2048,128]{1,0:T(8,128)S(1)}, u32[]{:S(2)}, u32[]{:S(2)}) collective-permute-start(f32[2048,128]{1,0:T(8,128)} %get-tuple-element.39), channel_id=1, source_target_pairs={{0,64},{64,0},{1,65},{65,1},{2,66},{66,2},{3,67},{67,3},{4,68},{68... | collective-permute-start | bytes 3145736 | tf_op jit(solution)/shard_map/ppermute | solution.py:265
Sparse Core Ops, SparseCore 0:
  12.4 24.4 sort.25.cloned.1.call-done
  (1 shorter events, 0.0 us)

commit v2 on v1

--- a/solution.py
+++ b/solution.py
@@ -6,7 +6,6 @@
 from jax.experimental import pallas as pl
 from jax.experimental.pallas import tpu as pltpu
 from jax.sharding import PartitionSpec as P
-
 
 DB = 128
 SB = 256
@@ -16,6 +15,7 @@
 BF = jnp.bfloat16
 F32 = jnp.float32
 VMEM_LIMIT = 60 << 20
+FRONT_LIMIT = 24 << 20
 
 
 def over(a, n):
@@ -31,7 +31,7 @@
 
 
 def product(a_ref, start, table_ref):
-    depth, _ = table_ref.shape
+    depth, width = table_ref.shape
     total = None
     for k in range(0, depth, SB):
         pieces = jnp.concatenate(split3(a_ref[pl.ds(start, DB), k : k + SB]), axis=0)
@@ -53,25 +53,11 @@
     return pltpu.make_async_copy(src.at[rows, :], dst.at[rows, :], sem.at[i])
 
 
-def multiply_kernel(a_hbm, table_ref, mine_ref, other_ref, a_ref, sem):
-    n_blocks = a_ref.shape[0] // DB
-
-    @pl.loop(0, n_blocks)
-    def _(i):
-        block_copy(a_hbm, a_ref, i, sem).start()
-
-    @pl.loop(0, n_blocks)
-    def _(i):
-        block_copy(a_hbm, a_ref, i, sem).wait()
-        write_product(a_ref, i, table_ref, mine_ref, other_ref)
-
-
-def build_kernel(first_block, kf_ref, kl_ref, begin_ref, key_ref, low_ref, w_ref, table_ref, a_hbm, mine_ref, other_ref, state_ref, a_ref, sem):
+def build_kernel(kf_ref, kl_ref, key_ref, low_ref, w_ref, table_ref, a_hbm, mine_ref, other_ref, a_ref, sem):
     n_src = a_ref.shape[1] // SB
     n_rows = key_ref.shape[0]
     n_blocks = a_ref.shape[0] // DB
-    first = first_block * n_src
-    limit = first + n_blocks * n_src
+    limit = n_blocks * n_src
 
     @pl.loop(0, n_blocks)
     def _(i):
@@ -96,7 +82,7 @@
                 jnp.concatenate(pieces, axis=0), s_hot, (((1,), (1,)), ((), ())), preferred_element_type=F32
             )
             got = got[:DB] + got[DB : 2 * DB] + got[2 * DB :]
-            place = jnp.clip(bucket - first, 0, n_blocks * n_src - 1)
+            place = jnp.minimum(bucket, limit - 1)
             block = place // n_src
             column = pl.multiple_of((place - block * n_src) * SB, SB)
             a_ref[pl.ds(pl.multiple_of(block * DB, DB), DB), pl.ds(column, SB)] += got
@@ -107,9 +93,7 @@
             bucket = jnp.where(live, next_bucket, bucket)
         return at, bucket
 
-    at, bucket = lax.while_loop(lambda c: c[1] < limit, body, (begin_ref[0], begin_ref[1]))
-    state_ref[0] = at
-    state_ref[1] = bucket
+    lax.while_loop(lambda c: c[1] < limit, body, (jnp.int32(0), kf_ref[0]))
 
     @pl.loop(0, n_blocks)
     def _(i):
@@ -129,40 +113,316 @@
 VMEM_SPEC = pl.BlockSpec(memory_space=pltpu.VMEM)
 
 
-def build_and_multiply(edges, begin, table, first_block, n_blocks):
-    k_first, k_last, keys, low, w = edges
+def build_and_multiply(edges, table, n_blocks):
     depth, full = table.shape
     rows = n_blocks * DB
     return pl.pallas_call(
-        functools.partial(build_kernel, first_block),
-        in_specs=[SMEM_SPEC] * 3 + [VMEM_SPEC] * 4,
-        out_specs=[HBM_SPEC, VMEM_SPEC, VMEM_SPEC, SMEM_SPEC],
+        build_kernel,
+        in_specs=[SMEM_SPEC] * 2 + [VMEM_SPEC] * 4,
+        out_specs=[HBM_SPEC, VMEM_SPEC, VMEM_SPEC],
         scratch_shapes=[pltpu.VMEM((rows, depth), F32), pltpu.SemaphoreType.DMA((n_blocks,))],
         out_shape=[
             jax.ShapeDtypeStruct((rows, depth), F32),
             jax.ShapeDtypeStruct((rows, full // 2), F32),
             jax.ShapeDtypeStruct((rows, full // 2), F32),
-            jax.ShapeDtypeStruct((2,), jnp.int32),
         ],
         compiler_params=pltpu.CompilerParams(vmem_limit_bytes=VMEM_LIMIT),
         cost_estimate=pl.CostEstimate(flops=n_blocks * 2 * 10**9, bytes_accessed=10**7, transcendentals=0),
         name="build_adjacency",
-    )(k_first, k_last, begin, keys, low, w, table)
-
-
-def multiply(a, table):
-    rows, depth = a.shape
-    full = table.shape[1]
+    )(*edges, table)
+
+
+MESH = pl.DeviceIdType.MESH
+
+
+def block(i, size):
+    return pl.ds(pl.multiple_of(i * size, size), size)
+
+
+def hot(condition):
+    return jnp.where(condition, 1.0, 0.0).astype(BF)
+
+
+def iota(shape, axis):
+    return lax.broadcasted_iota(jnp.int32, shape, axis)
+
+
+class Links:
+    def __init__(self, n_graph, send_sem, recv_sem):
+        self.n_graph, self.send_sem, self.recv_sem = n_graph, send_sem, recv_sem
+        self.me = lax.axis_index("graph")
+        self.col = lax.axis_index("feat")
+
+    def peer(self, k):
+        return lax.rem(self.me + k, self.n_graph)
+
+    def copy(self, kind, src, dst, device):
+        return pltpu.make_async_remote_copy(
+            src_ref=src,
+            dst_ref=dst,
+            send_sem=self.send_sem.at[kind],
+            recv_sem=self.recv_sem.at[kind],
+            device_id=device,
+            device_id_type=MESH,
+        )
+
+    def partner(self, kind, src, dst):
+        return self.copy(kind, src, dst, {"feat": 1 - self.col})
+
+    def announce(self, with_partner):
+        barrier = pltpu.get_barrier_semaphore()
+
+        @pl.loop(1, self.n_graph)
+        def _(k):
+            pl.semaphore_signal(barrier, inc=1, device_id={"graph": self.peer(k)}, device_id_type=MESH)
+
+        if with_partner:
+            pl.semaphore_signal(barrier, inc=1, device_id={"feat": 1 - self.col}, device_id_type=MESH)
+
+    def everyone_in(self, with_partner):
+        pl.semaphore_wait(pltpu.get_barrier_semaphore(), self.n_graph - 1 + int(with_partner))
+
+    def wait(self, kind, src, dst):
+        self.partner(kind, src, dst).wait()
+
+
+def send_rows(z_ref, wanted_ref, my_rows_ref, out_ref, hub_out_ref):
+    verts = z_ref.shape[0]
+
+    def pick(index):
+        parts = [hot(index == iota(index.shape, 1) + t * LANES) for t in range(verts // LANES)]
+        rows = jnp.concatenate(parts, axis=1)
+        return jnp.dot(rows, z_ref[...], preferred_element_type=F32).astype(BF)
+
+    hub_out_ref[...] = pick(my_rows_ref[...])
+    group = 2 * DB
+
+    @pl.loop(0, out_ref.shape[0] // group)
+    def _(i):
+        out_ref[block(i, group), :] = pick(wanted_ref[block(i, group), :])
+
+
+def start_rows(links, halo_kind, hub_kind, out_ref, hub_out_ref, table_ref, hub_in_ref, v_half):
+    own_hubs = hub_out_ref.shape[0]
+    s_half = out_ref.shape[0] // links.n_graph
+    here = table_ref.at[pl.ds(pl.multiple_of(v_half + links.me * s_half, s_half), s_half), :]
+    hub_here = hub_in_ref.at[block(links.me, own_hubs), :]
+
+    @pl.loop(1, links.n_graph)
+    def _(k):
+        peer = links.peer(k)
+        links.copy(halo_kind, out_ref.at[block(peer, s_half), :], here, {"graph": peer}).start()
+        links.copy(hub_kind, hub_out_ref, hub_here, {"graph": peer}).start()
+
+    here[...] = out_ref[block(links.me, s_half), :]
+    hub_here[...] = hub_out_ref[...]
+
+
+def finish_table(links, halo_kind, hub_kind, z_ref, out_ref, place_half_ref, table_ref, hub_in_ref, v_half):
+    others = links.n_graph - 1
+    s_half = out_ref.shape[0] // links.n_graph
+    own_hubs = hub_in_ref.shape[0] // links.n_graph
+    table_ref[0:v_half, :] = z_ref[pl.ds(pl.multiple_of(links.col * v_half, v_half), v_half), :]
+    hub_part = hub_in_ref.at[0 : others * own_hubs, :]
+    links.wait(hub_kind, hub_part, hub_part)
+    halo_part = table_ref.at[v_half : v_half + others * s_half, :]
+    links.wait(halo_kind, halo_part, halo_part)
+    hubs, k_half = hub_in_ref.shape[0], place_half_ref.shape[0]
+    index = place_half_ref[...]
+    rows = jnp.concatenate([hot(index == iota(index.shape, 1) + t * LANES) for t in range(hubs // LANES)], axis=1)
+    first = v_half + out_ref.shape[0]
+    table_ref[first : first + k_half, :] = jnp.dot(rows, hub_in_ref[...], preferred_element_type=F32).astype(BF)
+
+
+def front_kernel(n_graph, z_ref, wanted_ref, my_rows_ref, place_half_ref, result_ref, table_ref, out_ref, hub_out_ref, hub_in_ref, send_sem, recv_sem):
+    links = Links(n_graph, send_sem, recv_sem)
+    v_half = z_ref.shape[0] // 2
+    links.announce(False)
+    send_rows(z_ref, wanted_ref, my_rows_ref, out_ref, hub_out_ref)
+    links.everyone_in(False)
+    start_rows(links, 0, 1, out_ref, hub_out_ref, table_ref, hub_in_ref, v_half)
+    finish_table(links, 0, 1, z_ref, out_ref, place_half_ref, table_ref, hub_in_ref, v_half)
+    result_ref[...] = table_ref[...]
+
+
+def first_table(n_graph, z, wanted, my_rows, place_half, depth):
+    verts, full = z.shape
+    own_hubs = my_rows.shape[0]
     return pl.pallas_call(
-        multiply_kernel,
-        in_specs=[HBM_SPEC, VMEM_SPEC],
-        out_specs=[VMEM_SPEC] * 2,
-        scratch_shapes=[pltpu.VMEM((rows, depth), F32), pltpu.SemaphoreType.DMA((rows // DB,))],
-        out_shape=[jax.ShapeDtypeStruct((rows, full // 2), F32)] * 2,
-        compiler_params=pltpu.CompilerParams(vmem_limit_bytes=VMEM_LIMIT),
-        cost_estimate=pl.CostEstimate(flops=6 * rows * depth * full, bytes_accessed=10**7, transcendentals=0),
-        name="multiply_adjacency",
-    )(a, table)
+        functools.partial(front_kernel, n_graph),
+        in_specs=[VMEM_SPEC] * 4,
+        out_specs=VMEM_SPEC,
+        out_shape=jax.ShapeDtypeStruct((depth, full), BF),
+        scratch_shapes=[
+            pltpu.VMEM((depth, full), BF),
+            pltpu.VMEM((wanted.shape[0], full), BF),
+            pltpu.VMEM((own_hubs, full), BF),
+            pltpu.VMEM((n_graph * own_hubs, full), BF),
+            pltpu.SemaphoreType.DMA((2,)),
+            pltpu.SemaphoreType.DMA((2,)),
+        ],
+        compiler_params=pltpu.CompilerParams(collective_id=0, has_side_effects=True, vmem_limit_bytes=FRONT_LIMIT),
+        cost_estimate=pl.CostEstimate(flops=10**10, bytes_accessed=4 * 10**6, transcendentals=0),
+        name="first_table",
+    )(z, wanted, my_rows, place_half)
+
+
+def rest_kernel(
+    n_graph, sums_mine, sums_other, a_hbm, weights_ref, bias1_ref, bias2_ref, wanted_ref, my_rows_ref, my_line_ref,
+    place_half_ref, place_line_ref, result_ref,
+    a_ref, hub_rx, local_rx, pieces_ref, parts_ref, total_rx, total_ref, h_ref, h_rx, z_ref, out_ref, hub_out_ref, hub_in_ref,
+    table_ref, hub_mine, hub_other, local_other, hub_rx2, local_rx2, parts_ref2, total_rx2, a_sem, send_sem, recv_sem,
+):
+    links = Links(n_graph, send_sem, recv_sem)
+    hubs, width = hub_rx.shape
+    verts = result_ref.shape[0]
+    own_hubs = hubs // n_graph
+    v_half = verts // 2
+    n_hub_blocks = hubs // DB
+    n_local_blocks = verts // DB
+    tall = 2 * DB
+
+    @pl.loop(0, n_hub_blocks + n_local_blocks)
+    def _(i):
+        block_copy(a_hbm, a_ref, i, a_sem).start()
+
+    links.announce(True)
+    links.everyone_in(True)
+    hub_rows = sums_other.at[0:hubs, :]
+    local_rows = sums_other.at[hubs : hubs + verts, :]
+    links.partner(0, hub_rows, hub_rx).start()
+    links.partner(1, local_rows, local_rx).start()
+    total_ref[...] = jnp.zeros_like(total_ref)
+
+    def hub_exchange(kind, own, theirs, parts, arrivals):
+        @pl.loop(0, hubs // tall)
+        def _(i):
+            rows = block(i, tall)
+            pieces_ref[rows, :] = jnp.concatenate(split3(own[rows, :] + theirs[rows, :]), axis=1)
+
+        @pl.loop(0, hubs // tall)
+        def _(i):
+            rows = hot(place_line_ref[...] == iota((tall, hubs), 0) + i * tall)
+            got = jnp.dot(rows, pieces_ref[...], preferred_element_type=F32)
+            parts[block(i, tall), :] = got[:, :width] + got[:, width : 2 * width] + got[:, 2 * width :]
+
+        here = arrivals.at[block(links.me, own_hubs), :]
+
+        @pl.loop(1, n_graph)
+        def _(k):
+            peer = links.peer(k)
+            links.copy(kind, parts.at[block(peer, own_hubs), :], here, {"graph": peer}).start()
+
+        here[...] = parts[block(links.me, own_hubs), :]
+
+    def hub_total(kind, arrivals):
+        part = arrivals.at[0 : (n_graph - 1) * own_hubs, :]
+        links.wait(kind, part, part)
+        total = jnp.sum(arrivals[...].reshape(n_graph, own_hubs, width), axis=0)
+        total_ref[0:own_hubs, :] = jnp.concatenate(split3(total), axis=1)
+
+    def hub_add(i):
+        at = hot(my_line_ref[...] == iota((tall, LANES), 0) + i * tall)
+        got = jnp.dot(at, total_ref[...], preferred_element_type=F32)
+        return got[:, :width] + got[:, width : 2 * width] + got[:, 2 * width :]
+
+    links.wait(0, hub_rows, hub_rx)
+    hub_exchange(2, sums_mine, hub_rx, parts_ref, total_rx)
+    links.wait(1, local_rows, local_rx)
+    hub_total(2, total_rx)
+
+    @pl.loop(0, verts // tall)
+    def _(i):
+        rows = block(i, tall)
+        y = sums_mine[pl.ds(pl.multiple_of(hubs + i * tall, tall), tall), :] + local_rx[rows, :]
+        h_ref[rows, :] = jnp.maximum(y + hub_add(i) + bias1_ref[...], 0.0).astype(BF)
+
+    links.partner(3, h_ref, h_rx).start()
+    links.wait(3, h_ref, h_rx)
+
+    @pl.loop(0, verts // tall)
+    def _(i):
+        rows = block(i, tall)
+        z = jnp.dot(h_ref[rows, :], weights_ref[0:width, :], preferred_element_type=F32)
+        z = z + jnp.dot(h_rx[rows, :], weights_ref[width : 2 * width, :], preferred_element_type=F32)
+        z_ref[rows, :] = z.astype(BF)
+
+    send_rows(z_ref, wanted_ref, my_rows_ref, out_ref, hub_out_ref)
+    start_rows(links, 4, 5, out_ref, hub_out_ref, table_ref, hub_in_ref, v_half)
+    finish_table(links, 4, 5, z_ref, out_ref, place_half_ref, table_ref, hub_in_ref, v_half)
+
+    @pl.loop(0, n_hub_blocks)
+    def _(i):
+        block_copy(a_hbm, a_ref, i, a_sem).wait()
+        y = product(a_ref, pl.multiple_of(i * DB, DB), table_ref)
+        hub_mine[block(i, DB), :] = y[:, :width]
+        hub_other[block(i, DB), :] = y[:, width:]
+
+    links.partner(6, hub_other, hub_rx2).start()
+    links.wait(6, hub_other, hub_rx2)
+    hub_exchange(7, hub_mine, hub_rx2, parts_ref2, total_rx2)
+
+    @pl.loop(0, n_local_blocks)
+    def _(i):
+        block_copy(a_hbm, a_ref, i + n_hub_blocks, a_sem).wait()
+        y = product(a_ref, pl.multiple_of(hubs + i * DB, DB), table_ref)
+        rows = block(i, DB)
+        result_ref[rows, :] = y[:, :width]
+        local_other[rows, :] = y[:, width:]
+
+    links.partner(8, local_other, local_rx2).start()
+    hub_total(7, total_rx2)
+    links.wait(8, local_other, local_rx2)
+
+    @pl.loop(0, verts // tall)
+    def _(i):
+        rows = block(i, tall)
+        result_ref[rows, :] = result_ref[rows, :] + local_rx2[rows, :] + hub_add(i) + bias2_ref[...]
+
+
+def rest(n_graph, sums_mine, sums_other, adjacency, weights, bias1, bias2, wanted, my_rows, my_line, place_half, place_line):
+    rows, depth = adjacency.shape
+    hubs = place_line.shape[1]
+    verts = rows - hubs
+    width = bias1.shape[1]
+    full = 2 * width
+    own_hubs = hubs // n_graph
+    half_rows = lambda n: pltpu.VMEM((n, width), F32)
+    return pl.pallas_call(
+        functools.partial(rest_kernel, n_graph),
+        in_specs=[VMEM_SPEC, VMEM_SPEC, HBM_SPEC] + [VMEM_SPEC] * 8,
+        out_specs=VMEM_SPEC,
+        out_shape=jax.ShapeDtypeStruct((verts, width), F32),
+        scratch_shapes=[
+            pltpu.VMEM((rows, depth), F32),
+            half_rows(hubs),
+            half_rows(verts),
+            pltpu.VMEM((hubs, 3 * width), BF),
+            half_rows(hubs),
+            half_rows(hubs),
+            pltpu.VMEM((LANES, 3 * width), BF),
+            pltpu.VMEM((verts, width), BF),
+            pltpu.VMEM((verts, width), BF),
+            pltpu.VMEM((verts, full), BF),
+            pltpu.VMEM((wanted.shape[0], full), BF),
+            pltpu.VMEM((own_hubs, full), BF),
+            pltpu.VMEM((hubs, full), BF),
+            pltpu.VMEM((depth, full), BF),
+            half_rows(hubs),
+            half_rows(hubs),
+            half_rows(verts),
+            half_rows(hubs),
+            half_rows(verts),
+            half_rows(hubs),
+            half_rows(hubs),
+            pltpu.SemaphoreType.DMA((rows // DB,)),
+            pltpu.SemaphoreType.DMA((9,)),
+            pltpu.SemaphoreType.DMA((9,)),
+        ],
+        compiler_params=pltpu.CompilerParams(collective_id=1, has_side_effects=True, vmem_limit_bytes=VMEM_LIMIT),
+        cost_estimate=pl.CostEstimate(flops=2 * 10**10, bytes_accessed=4 * 10**7, transcendentals=0),
+        name="rest",
+    )(sums_mine, sums_other, adjacency, weights, bias1, bias2, wanted, my_rows, my_line, place_half, place_line)
 
 
 def solution(mesh):
@@ -227,56 +487,23 @@
         earlier = (owner[None, :] == owner[:, None]) & (ids[None, :] < ids[:, None])
         place = owner * own_hubs + jnp.sum(earlier.astype(jnp.int32), axis=1)
         place_half = lax.dynamic_slice_in_dim(place, col * k_half, k_half)
-        hub_hot = (place_half[:, None] == ids[None, :]).astype(BF)
-        hub_hot_t = (place[None, :] == ids[:, None]).astype(BF)
         slot_ids = me * own_hubs + jnp.arange(own_hubs)
         my_rows = jnp.sum(jnp.where(place[None, :] == slot_ids[:, None], hub_ids[None, :], 0), axis=1) - me * verts
-
+        my_line = jnp.pad(my_rows, (0, LANES - own_hubs), constant_values=-1)[None, :]
         wanted = jnp.where(send_valid > 0, send_idx, -1)
-        wanted = lax.dynamic_slice_in_dim(wanted, col * s_half, s_half, 1)
-        wanted = jnp.concatenate([wanted, jnp.broadcast_to(my_rows[None, :], (n_graph, own_hubs))], axis=1)
-        wanted = wanted.reshape(-1)
-        send_hot = (wanted[:, None] == jnp.arange(verts)[None, :]).astype(BF)
-
-        def table_of(mine, weights):
-            other = lax.ppermute(mine, "feat", swap)
-            z = jnp.dot(mine, weights[0], preferred_element_type=F32)
-            z = (z + jnp.dot(other, weights[1], preferred_element_type=F32)).astype(BF)
-            out = jnp.dot(send_hot, z, preferred_element_type=F32).astype(BF)
-            got = lax.all_to_all(out.reshape(n_graph, s_half + own_hubs, 2 * width), "graph", 0, 0, tiled=True)
-            hub_rows = got[:, s_half:].reshape(hubs, 2 * width)
-            hub_rows = jnp.dot(hub_hot, hub_rows, preferred_element_type=F32).astype(BF)
-            own = lax.dynamic_slice_in_dim(z, col * v_half, v_half)
-            return jnp.concatenate([own, got[:, :s_half].reshape(n_graph * s_half, 2 * width), hub_rows], axis=0)
-
-        def hub_parts(mine, other):
-            sums = mine + lax.ppermute(other, "feat", swap)
-            hi = lax.reduce_precision(sums, 8, 7)
-            mid = lax.reduce_precision(sums - hi, 8, 7)
-            pieces = jnp.concatenate([hi.astype(BF), mid.astype(BF), ((sums - hi) - mid).astype(BF)], axis=1)
-            got = jnp.dot(hub_hot_t, pieces, preferred_element_type=F32)
-            return got[:, :width] + got[:, width : 2 * width] + got[:, 2 * width :]
-
-        def hub_total(parts):
-            got = lax.all_to_all(parts.reshape(n_graph, own_hubs, width), "graph", 0, 0, tiled=True)
-            return jnp.sum(got, axis=0)
-
-        def finish(mine, other, total, bias):
-            return (mine + lax.ppermute(other, "feat", swap) + bias).at[my_rows].add(total)
-
-        table = table_of(x_loc, w1)
-        begin = jnp.stack([jnp.int32(0), k_first[0]])
-        a_hub, mine, other, state = build_and_multiply(edges, begin, table, 0, hub_blocks)
-        parts, state = lax.optimization_barrier((hub_parts(mine, other), state))
-        total = hub_total(parts)
-        a_local, mine, other, _ = build_and_multiply(edges, state, table, hub_blocks, local_blocks)
-        hidden = jnp.maximum(finish(mine, other, total, b_first), 0.0).astype(BF)
-
-        table = table_of(hidden, w2)
-        parts, table_local = lax.optimization_barrier((hub_parts(*multiply(a_hub, table)), table))
-        total = hub_total(parts)
-        mine, other = multiply(a_local, table_local)
-        return finish(mine, other, total, b_second)
+        wanted = lax.dynamic_slice_in_dim(wanted, col * s_half, s_half, 1).reshape(-1)
+        across = lambda a: jnp.broadcast_to(a[:, None], (a.shape[0], LANES))
+        lists = (across(wanted), across(my_rows))
+
+        z = jnp.dot(x_loc, w1[0], preferred_element_type=F32)
+        z = (z + jnp.dot(lax.ppermute(x_loc, "feat", swap), w1[1], preferred_element_type=F32)).astype(BF)
+        table = first_table(n_graph, z, *lists, across(place_half), depth)
+        adjacency, mine, other = build_and_multiply(edges, table, hub_blocks + local_blocks)
+        weights = jnp.concatenate(w2, axis=0)
+        return rest(
+            n_graph, mine, other, adjacency, weights, b_first[None, :], b_second[None, :],
+            *lists, my_line, across(place_half), place[None, :],
+        )
 
     edge = P(rows_axes)
     send = P(rows_axes, None)

time: 230 us -> 185 us (0.80)
  Pallas kernels: 80.5 us -> 152 us
  waiting for transfers between devices: 57.7 us -> 0.01 us
  starting transfers between devices: 22.8 us -> 0.75 us
  blocking collectives: 18.4 us -> 0 us
  matrix products: 13 us -> 0.97 us
  other arithmetic: 16.1 us -> 4.53 us
  local copies, waits for them, and re-layouts: 5.8 us -> 9.73 us
    pallas_call x4 -> x3, Pallas kernels: 80.5 us -> 152 us  [the longest x1 72.1 us: rest(): pl.pallas_call(functools.partial(rest_kernel, n_graph), in_specs=[VMEM_SP...]
    all_to_all x3 -> x0, waiting for transfers between devices: 52.1 us -> none  [the longest x2 38.4 us: table_of(): lax.all_to_all(out.reshape(n_graph, s_half + own_hubs, 2 * width), 'graph...]
    all_to_all x3 -> x0, starting transfers between devices: 21.2 us -> none  [the longest x2 16.2 us: table_of(): lax.all_to_all(out.reshape(n_graph, s_half + own_hubs, 2 * width), 'graph...]
    all_to_all x1 -> x0, blocking collectives: 18.4 us -> none  [hub_total(): lax.all_to_all(parts.reshape(n_graph, own_hubs, width), 'graph', 0, 0, ti...]
    dot_general x10 -> x2, matrix products: 13 us -> 0.97 us  [the longest x1 0.48 us: device_program(): z = jnp.dot(x_loc, w1[0], preferred_element_type=F32)]
    ppermute x6 -> x1, waiting for transfers between devices: 5.67 us -> 0.01 us  [device_program(): lax.ppermute(x_loc, 'feat', swap)]
    scatter-add x2 -> x0, other arithmetic: 3.85 us -> none  [finish(): (mine + lax.ppermute(other, 'feat', swap) + bias).at[my_rows].add(total)]
    unnamed x21 -> x22, local copies, waits for them, and re-layouts: 0.2 us -> 3.38 us
  transfers between devices with their start and end apart: 11 -> 3, of which waited for: 6 -> 0; matrix products, arithmetic and copies ran while one was open for 3% -> 4% of each run, Pallas kernels for 0% -> 0%
where the time goes in v2:
time: 185 us; the launch traced here: 182 us
  Pallas kernels  152 us (82%)
  between operations  13.7 us (7%)
  local copies, waits for them, and re-layouts  9.73 us (5%)
  other arithmetic  4.53 us (2%)
    pallas_call x1, Pallas kernels, rest(): pl.pallas_call(functools.partial(rest_kernel, n_graph), in_specs=[VMEM_SP...  72.1 us
    pallas_call x1, Pallas kernels, build_and_multiply(): pl.pallas_call(build_kernel, in_specs=[SMEM_SPEC] * 2 + [VMEM_SPEC] * 4,...  55 us
    pallas_call x1, Pallas kernels, first_table(): pl.pallas_call(functools.partial(front_kernel, n_graph), in_specs=[VMEM_S...  25.2 us
  transfers between devices with their start and end apart: 3, of which 0 were waited for; matrix products, arithmetic and copies ran while one was open for 4% of the time, Pallas kernels for 0%

profile of v2, /device:TPU:0, one launch (start us, length us, event | category | flops | bytes accessed | tf_op | source)
XLA Modules:
  0.0 181.9 jit_solution(2066519289072840659)
XLA Ops:
  6.5 0.0 sort.23.cloned.1.call-start
  6.5 0.7 constant_dynamic-slice_fusion.3
  7.3 0.0 copy-start.4
  7.3 0.1 collective-permute-start
  7.4 0.5 collective-permute-start.1
  7.9 0.8 constant_dynamic-slice_fusion
  8.7 0.2 collective-permute-start.2
  8.8 1.7 and_add_fusion
  10.6 0.0 copy-start.6
  10.6 0.0 copy-start.8
  10.6 0.0 copy-start.9
  10.6 0.0 copy-start.5
  10.6 0.8 pad.18
  11.5 0.8 pad.17
  12.3 0.0 copy-done.4
  12.3 0.8 pad.19
  13.1 0.0 sort.23.cloned.1.call-update
  13.1 0.0 copy-done.6
  13.2 0.0 copy-done.8
  13.2 0.0 copy-done.9
  13.2 0.5 convert_reduce_fusion
  13.8 0.0 copy-start.7
  13.8 0.2 select_reduce_fusion
  14.0 0.0 copy-done.5
  14.0 0.5 fusion.7
  14.5 0.5 pad_bitcast_fusion.my_line_ref
  15.0 0.1 dynamic_slice.21
  15.1 0.1 copy.20
  15.1 0.1 broadcast_in_dim.64
  15.2 0.0 collective-permute-done
  15.2 0.0 collective-permute-done.2
  15.3 0.7 maximum_maximum_fusion.weights_ref
  15.9 0.0 collective-permute-done.1
  15.9 0.5 fusion.2.z_ref
  16.4 0.0 copy-done.7
  16.4 0.1 broadcast_in_dim.69.place_half_ref
  16.6 0.0 copy-start.1
  16.6 0.2 broadcast_in_dim.65.wanted_ref
  16.8 0.0 copy-start
  16.8 0.1 broadcast_in_dim.68.my_rows_ref
  16.8 0.0 copy-start.2
  16.9 25.2 %first_table.1.table_ref = bf16[2560,256]{1,0:T(8,128)(2,1)S(1)} custom-call(bf16[2048,256]{1,0:T(8,128)(2,1)S(1)} %fusion.2.z_ref, s32[1024,128]{1,0:T(8,128)S(1)} %broadcast_in_dim.65.wanted_ref, s32[16,128]{1,0:T(8,128)S(1)} %broadcast_in_dim.68.my_rows_ref, s32[512,128]{1,0:T(8,128)S(1)} %broadcast_in_dim.69.place_half_ref), custom_call_target="tpu_custom_call" | custom-call | flops 10000000000 | bytes 4000000 | tf_op jit(solution)/shard_map/first_table/pallas_call | solution.py:251
  42.0 0.0 copy-done.1
  42.0 0.0 copy-done
  42.1 0.0 copy-done.2
  42.1 0.0 copy-start.3
  42.1 1.0 copy-done.3
  43.1 0.0 sort.23.cloned.1.call-done
  43.1 1.4 bitcast_reduce_fusion
  44.5 0.6 concatenate.21.kf_ref
  45.1 0.6 concatenate.22.kl_ref
  45.7 55.0 %build_adjacency.1 = (f32[3072,2560]{1,0:T(8,128)}, f32[3072,128]{1,0:T(8,128)}, f32[3072,128]{1,0:T(8,128)}) custom-call(s32[1032]{0:T(1024)} %concatenate.21.kf_ref, s32[1032]{0:T(1024)} %concatenate.22.kl_ref, s32[1024,1,128]{2,1,0:T(1,128)} %bitcast.15, s32[1024,1,128]{2,1,0:T(1,128)} %bitcast.17, f32[1024,1,128]{2,1,0:T(1,128)} %bitcast.18, ...), custom_call_target="tpu_custom_call" | custom-call | flops 48000000000 | bytes 10000000 | tf_op jit(solution)/shard_map/build_adjacency/pallas_call | solution.py:119
  100.7 72.1 %rest.1 = f32[2048,128]{1,0:T(8,128)} custom-call(f32[3072,128]{1,0:T(8,128)} %get-tuple-element.14.sums_mine, f32[3072,128]{1,0:T(8,128)} %get-tuple-element.15.sums_other, f32[3072,2560]{1,0:T(8,128)} %get-tuple-element.16.a_hbm, bf16[256,256]{1,0:T(8,128)(2,1)} %maximum_maximum_fusion.weights_ref, f32[1,128]{1,0:T(1,128)} %bitcast.19, f32[1,128]{1,0:T(1,128)} %bitcast.20, ...), custom_call_target="tpu_custom_call" | custom-call | flops 20000000000 | bytes 40000000 | tf_op jit(solution)/shard_map/rest/pallas_call | solution.py:391
  172.8 2.3 %copy.24 = f32[2048,128]{1,0:T(8,128)} copy(f32[2048,128]{1,0:T(8,128)} %rest.1) | data formatting | bytes 2097152
  (9 shorter events, 0.1 us)
Async XLA Ops:
  6.5 36.6 %sort.23.cloned.1.call-start = ((), (), s32[]{:S(2)}) async-start(), calls=%async_computation | async-start | bytes 4718624 | tf_op jit(solution)/shard_map/sort | solution.py:477
  7.3 5.0 %copy-start.4 = (f32[102400]{0:T(1024)S(1)}, f32[102400]{0:T(1024)}, u32[]{:S(2)}) copy-start(f32[102400]{0:T(1024)} %param.16) | copy-start | bytes 1228804
  7.3 7.9 %collective-permute-start = (bf16[50,256]{1,0:T(8,128)(2,1)S(1)}, bf16[50,256]{1,0:T(8,128)(2,1)S(1)}, u32[]{:S(2)}, u32[]{:S(2)}) collective-permute-start(bf16[50,256]{1,0:T(8,128)(2,1)S(1)} %pad_maximum_fusion.1), channel_id=1, source_target_pairs={{0,64},{64,0},{1,65},{65,1},{2,66},{66,2},{3,67},{67,3},{4,68},{68... | collective-permute-start | bytes 76808 | tf_op jit(solution)/shard_map/ppermute | solution.py:451
  7.4 8.5 %collective-permute-start.1 = (bf16[2048,50]{0,1:T(8,128)(2,1)}, bf16[2048,50]{0,1:T(8,128)(2,1)S(1)}, u32[]{:S(2)}, u32[]{:S(2)}) collective-permute-start(bf16[2048,50]{0,1:T(8,128)(2,1)} %param.12), channel_id=1, source_target_pairs={{0,64},{64,0},{1,65},{65,1},{2,66},{66,2},{3,67},{67,3},{4,68},{68... | collective-permute-start | bytes 614408 | tf_op jit(solution)/shard_map/ppermute | solution.py:499
  8.7 6.6 %collective-permute-start.2 = (bf16[128,256]{1,0:T(8,128)(2,1)S(1)}, bf16[128,256]{1,0:T(8,128)(2,1)S(1)}, u32[]{:S(2)}, u32[]{:S(2)}) collective-permute-start(bf16[128,256]{1,0:T(8,128)(2,1)S(1)} %pad_maximum_fusion), channel_id=1, source_target_pairs={{0,64},{64,0},{1,65},{65,1},{2,66},{66,2},{3,67},{67,3},{4,68},{68... | collective-permute-start | bytes 196616 | tf_op jit(solution)/shard_map/ppermute | solution.py:451
  10.6 2.6 %copy-start.6 = (s32[1024]{0:T(1024)S(1)}, s32[1024]{0:T(1024)}, u32[]{:S(2)}) copy-start(s32[1024]{0:T(1024)} %param.19) | copy-start | bytes 12292
  10.6 2.6 %copy-start.8 = (s32[64,32]{0,1:T(8,128)S(1)}, s32[64,32]{0,1:T(8,128)}, u32[]{:S(2)}) copy-start(s32[64,32]{0,1:T(8,128)} %param.17) | copy-start | bytes 24580
  10.6 2.6 %copy-start.9 = (s32[64,32]{0,1:T(8,128)S(1)}, s32[64,32]{0,1:T(8,128)}, u32[]{:S(2)}) copy-start(s32[64,32]{0,1:T(8,128)} %param.18) | copy-start | bytes 24580
  10.6 3.4 %copy-start.5 = (bf16[2048,50]{0,1:T(8,128)(2,1)S(1)}, bf16[2048,50]{0,1:T(8,128)(2,1)}, u32[]{:S(2)}) copy-start(bf16[2048,50]{0,1:T(8,128)(2,1)} %param.12) | copy-start | bytes 614404
  13.8 2.7 %copy-start.7 = (s32[1024]{0:T(1024)}, s32[1024]{0:T(1024)S(1)}, u32[]{:S(2)}) copy-start(s32[1024]{0:T(1024)S(1)} %multiply_add_fusion) | copy-start | bytes 12292
  16.6 25.5 %copy-start.1 = (s32[512,128]{1,0:T(8,128)}, s32[512,128]{1,0:T(8,128)S(1)}, u32[]{:S(2)}) copy-start(s32[512,128]{1,0:T(8,128)S(1)} %broadcast_in_dim.69.place_half_ref) | copy-start | bytes 786436
  16.8 25.3 %copy-start = (s32[1024,128]{1,0:T(8,128)}, s32[1024,128]{1,0:T(8,128)S(1)}, u32[]{:S(2)}) copy-start(s32[1024,128]{1,0:T(8,128)S(1)} %broadcast_in_dim.65.wanted_ref) | copy-start | bytes 1572868
  16.8 25.2 %copy-start.2 = (s32[16,128]{1,0:T(8,128)}, s32[16,128]{1,0:T(8,128)S(1)}, u32[]{:S(2)}) copy-start(s32[16,128]{1,0:T(8,128)S(1)} %broadcast_in_dim.68.my_rows_ref) | copy-start | bytes 24580
  42.1 1.1 copy-start.3
Sparse Core Ops, SparseCore 0:
  13.3 24.6 sort.25.cloned.1.call-done
  (1 shorter events, 0.0 us)
